TPU v7x, 8 devices: a whole 2x2x1 slice. The times are simulated.
8 devices in a mesh: col: 2 (over z, y), row: 4 (over x, core).
Axes of the slice: x: 2, y: 2, z: 1, core: 2. Of those that a mesh axis runs over, the one named last changes fastest.
Arguments:
- forcing: float32 [192, 96, 256], P('row', 'col')
- u_init: float32 [192, 96, 256], P('row', 'col')
- diffusivity: float32 [192, 96], P('row', 'col')
- local_solve: bfloat16 [4, 2, 4096, 4096], P('row', 'col')
- relax_omega: float32 [], replicated
Outputs:
- output: float32 [192, 96, 256], P('row', 'col')
All inputs are finite; a program needn't handle non-finite values.
Results may differ from a plain program's by a relative error of at most 0.001.
Values are sent between devices in bfloat16 or wider.
A program may use at most 1 GiB of HBM per device.

v0:
```python
import math
import jax
import jax.numpy as jnp
from jax import lax
from jax.sharding import PartitionSpec as P

SWEEPS = 4


def from_lower(tile_block, axis_name, axis_count):
    return lax.ppermute(tile_block, axis_name, [(source, source + 1) for source in range(axis_count - 1)])


def from_upper(tile_block, axis_name, axis_count):
    return lax.ppermute(tile_block, axis_name, [(source + 1, source) for source in range(axis_count - 1)])


def solution(mesh):
    rows_dev = mesh.shape['row']
    cols_dev = mesh.shape['col']

    def grow_rows(tile_block, halo_width):
        extent = tile_block.shape[0]
        upper_rows = from_lower(tile_block[extent - halo_width:], 'row', rows_dev)
        lower_rows = from_upper(tile_block[:halo_width], 'row', rows_dev)
        return jnp.concatenate([upper_rows, tile_block, lower_rows], axis=0)

    def grow_cols(tile_block, halo_width):
        extent = tile_block.shape[1]
        left_cols = from_lower(tile_block[:, extent - halo_width:], 'col', cols_dev)
        right_cols = from_upper(tile_block[:, :halo_width], 'col', cols_dev)
        return jnp.concatenate([left_cols, tile_block, right_cols], axis=1)

    def fold_rows(tile_block, margin):
        tile_n = tile_block.shape[0] - 2 * margin
        from_above = from_lower(tile_block[margin + tile_n:], 'row', rows_dev)
        from_below = from_upper(tile_block[:margin], 'row', rows_dev)
        return (tile_block[margin:margin + tile_n]
                + jnp.pad(from_above, ((0, tile_n - margin), (0, 0), (0, 0)))
                + jnp.pad(from_below, ((tile_n - margin, 0), (0, 0), (0, 0))))

    def fold_cols(tile_block, margin):
        tile_n = tile_block.shape[1] - 2 * margin
        from_left = from_lower(tile_block[:, margin + tile_n:], 'col', cols_dev)
        from_right = from_upper(tile_block[:, :margin], 'col', cols_dev)
        return (tile_block[:, margin:margin + tile_n]
                + jnp.pad(from_left, ((0, 0), (0, tile_n - margin), (0, 0)))
                + jnp.pad(from_right, ((0, 0), (tile_n - margin, 0), (0, 0))))

    def apply_operator(grid_field, weight_x, weight_y):
        tall_field = grow_rows(grid_field, 1)
        wide_field = grow_cols(grid_field, 1)
        return (weight_x[:-1, :, None] * (grid_field - tall_field[:-2])
                + weight_x[1:, :, None] * (grid_field - tall_field[2:])
                + weight_y[:, :-1, None] * (grid_field - wide_field[:, :-2])
                + weight_y[:, 1:, None] * (grid_field - wide_field[:, 2:]))

    def local_step(forcing, u_init, diffusivity, local_solve, relax_omega):
        tile_n = forcing.shape[0]
        num_rhs = forcing.shape[2]
        ext_n = math.isqrt(local_solve.shape[-1])
        margin = (ext_n - tile_n) // 2
        matrix = local_solve[0, 0]
        kappa_tall = grow_rows(diffusivity, 1)
        kappa_wide = grow_cols(diffusivity, 1)
        weight_x = 0.5 * (kappa_tall[:-1] + kappa_tall[1:])
        weight_y = 0.5 * (kappa_wide[:, :-1] + kappa_wide[:, 1:])
        residual = forcing - apply_operator(u_init, weight_x, weight_y)
        solution_u = u_init
        for sweep_index in range(SWEEPS):
            window = grow_cols(grow_rows(residual.astype(jnp.bfloat16), margin), margin)
            solved = jnp.dot(matrix, window.reshape(ext_n * ext_n, num_rhs), preferred_element_type=jnp.float32)
            update = fold_rows(fold_cols(solved.reshape(ext_n, ext_n, num_rhs), margin), margin)
            solution_u = solution_u + relax_omega * update
            if sweep_index < SWEEPS - 1:
                residual = residual - relax_omega * apply_operator(update, weight_x, weight_y)
        return solution_u

    field_spec = P('row', 'col', None)
    return jax.shard_map(local_step, mesh=mesh,
                         in_specs=(field_spec, field_spec, P('row', 'col'), P('row', 'col', None, None), P()),
                         out_specs=field_spec, check_vma=False)
```

profile of v0, /device:TPU:0, one launch (start us, length us, event | category | flops | bytes accessed | tf_op | source)
XLA Modules:
  0.0 375.6 jit_solution(14500113670331912200)
XLA Ops:
  7.6 4.9 %collective-permute-start.4 = (f32[48,1]{1,0:T(8,128)S(1)}, f32[48,1]{1,0:T(8,128)S(1)}, u32[]{:S(2)}, u32[]{:S(2)}) collective-permute-start(f32[48,1]{1,0:T(8,128)S(1)} %get-tuple-element.66), channel_id=1, source_target_pairs={{0,4},{1,5},{2,6},{3,7}} | collective-permute-start | bytes 584 | tf_op jit(solution)/shard_map/ppermute | solution.py:11
  25.3 9.5 %fusion.88 = (bf16[48,48,256]{2,1,0:T(8,128)(2,1)S(1)}, f32[48,48,256]{2,1,0:T(8,128)}) fusion(f32[48,48,256]{2,1,0:T(8,128)} %param.5, f32[48,48,256]{2,1,0:T(8,128)} %param.6, f32[48,1,256]{2,1,0:T(1,128)S(1)} %collective-permute-done.7, f32[48,48]{1,0:T(8,128)S(1)} %get-tuple-element.64, f32[48,1,256]{2,1,0:T(1,128)S(1)} %collective-permute-done.6, ...), kind=kLoop, calls=%fused_computation.120 | loop fusion | flops 10027008 | bytes 8491008 | tf_op jit(solution)/shard_map/convert_element_type | solution.py:71
  51.4 4.7 %collective-permute-done.11 = bf16[64,8,256]{2,1,0:T(8,128)(2,1)S(1)} collective-permute-done((bf16[64,8,256]{2,1,0:T(8,128)(2,1)S(1)}, bf16[64,8,256]{2,1,0:T(8,128)(2,1)S(1)}, u32[]{:S(2)}, u32[]{:S(2)}) %collective-permute-start.11) | collective-permute-done | bytes 262176 | tf_op jit(solution)/shard_map/ppermute | solution.py:15
  56.6 16.4 %fusion.8 = f32[4096,256]{0,1:T(8,128)} fusion(bf16[4096,256]{1,0:T(8,128)(2,1)S(1)} %bitcast.45, bf16[1,1,4096,4096]{3,2,1,0:T(8,128)(2,1)} %param.8), kind=kOutput, calls=%fused_computation.8 | convolution fusion | flops 8589934592 | bytes 39845888 | tf_op jit(solution)/shard_map/dot_general | solution.py:72
  73.1 5.7 %copy.18 = f32[4096,256]{1,0:T(8,128)} copy(f32[4096,256]{0,1:T(8,128)} %fusion.8) | data formatting | bytes 8388608 | tf_op jit(solution)/shard_map/dot_general | solution.py:72
  82.8 9.4 %collective-permute-done.12 = f32[64,8,256]{2,1,0:T(8,128)S(1)} collective-permute-done((f32[64,8,256]{2,1,0:T(8,128)S(1)}, f32[64,8,256]{2,1,0:T(8,128)S(1)}, u32[]{:S(2)}, u32[]{:S(2)}) %collective-permute-start.12) | collective-permute-done | bytes 524320 | tf_op jit(solution)/shard_map/ppermute | solution.py:11
  92.2 4.7 %collective-permute-done.13 = f32[64,8,256]{2,1,0:T(8,128)S(1)} collective-permute-done((f32[64,8,256]{2,1,0:T(8,128)S(1)}, f32[64,8,256]{2,1,0:T(8,128)S(1)}, u32[]{:S(2)}, u32[]{:S(2)}) %collective-permute-start.13) | collective-permute-done | bytes 524320 | tf_op jit(solution)/shard_map/ppermute | solution.py:15
  109.2 7.1 %collective-permute-start.16 = (f32[1,48,256]{2,1,0:T(8,128)S(1)}, f32[1,48,256]{2,1,0:T(8,128)S(1)}, u32[]{:S(2)}, u32[]{:S(2)}) collective-permute-start(f32[1,48,256]{2,1,0:T(8,128)S(1)} %get-tuple-element.35), channel_id=1, source_target_pairs={{0,1},{1,2},{2,3},{4,5},{5,6},{6,7}} | collective-permute-start | bytes 147464 | tf_op jit(solution)/shard_map/ppermute | solution.py:11
  119.4 5.1 %fusion.86 = (bf16[48,48,256]{2,1,0:T(8,128)(2,1)S(1)}, f32[48,48,256]{2,1,0:T(8,128)}) fusion(f32[48,48,256]{2,1,0:T(8,128)} %get-tuple-element.10, f32[48,48,256]{2,1,0:T(8,128)S(1)} %fusion.69, f32[48,1,256]{2,1,0:T(1,128)S(1)} %collective-permute-done.19, f32[48,48]{1,0:T(8,128)S(1)} %get-tuple-element.64, ...), kind=kLoop, calls=%fused_computation.119 | loop fusion | flops 10616832 | bytes 8491012 | tf_op jit(solution)/shard_map/convert_element_type | solution.py:71
  140.8 4.7 %collective-permute-done.23 = bf16[64,8,256]{2,1,0:T(8,128)(2,1)S(1)} collective-permute-done((bf16[64,8,256]{2,1,0:T(8,128)(2,1)S(1)}, bf16[64,8,256]{2,1,0:T(8,128)(2,1)S(1)}, u32[]{:S(2)}, u32[]{:S(2)}) %collective-permute-start.23) | collective-permute-done | bytes 262176 | tf_op jit(solution)/shard_map/ppermute | solution.py:15
  146.0 16.4 %fusion.11 = f32[4096,256]{0,1:T(8,128)} fusion(bf16[4096,256]{1,0:T(8,128)(2,1)S(1)} %bitcast.46, bf16[1,1,4096,4096]{3,2,1,0:T(8,128)(2,1)} %param.8), kind=kOutput, calls=%fused_computation.9 | convolution fusion | flops 8589934592 | bytes 39845888 | tf_op jit(solution)/shard_map/dot_general | solution.py:72
  162.4 5.7 %copy.19 = f32[4096,256]{1,0:T(8,128)} copy(f32[4096,256]{0,1:T(8,128)} %fusion.11) | data formatting | bytes 8388608 | tf_op jit(solution)/shard_map/dot_general | solution.py:72
  172.2 9.4 %collective-permute-done.24 = f32[64,8,256]{2,1,0:T(8,128)S(1)} collective-permute-done((f32[64,8,256]{2,1,0:T(8,128)S(1)}, f32[64,8,256]{2,1,0:T(8,128)S(1)}, u32[]{:S(2)}, u32[]{:S(2)}) %collective-permute-start.24) | collective-permute-done | bytes 524320 | tf_op jit(solution)/shard_map/ppermute | solution.py:11
  181.6 4.7 %collective-permute-done.25 = f32[64,8,256]{2,1,0:T(8,128)S(1)} collective-permute-done((f32[64,8,256]{2,1,0:T(8,128)S(1)}, f32[64,8,256]{2,1,0:T(8,128)S(1)}, u32[]{:S(2)}, u32[]{:S(2)}) %collective-permute-start.25) | collective-permute-done | bytes 524320 | tf_op jit(solution)/shard_map/ppermute | solution.py:15
  198.9 7.1 %collective-permute-start.28 = (f32[1,48,256]{2,1,0:T(8,128)S(1)}, f32[1,48,256]{2,1,0:T(8,128)S(1)}, u32[]{:S(2)}, u32[]{:S(2)}) collective-permute-start(f32[1,48,256]{2,1,0:T(8,128)S(1)} %get-tuple-element.31), channel_id=1, source_target_pairs={{0,1},{1,2},{2,3},{4,5},{5,6},{6,7}} | collective-permute-start | bytes 147464 | tf_op jit(solution)/shard_map/ppermute | solution.py:11
  234.2 16.4 %fusion.14 = f32[4096,256]{0,1:T(8,128)} fusion(bf16[4096,256]{1,0:T(8,128)(2,1)S(1)} %bitcast.47, bf16[1,1,4096,4096]{3,2,1,0:T(8,128)(2,1)} %param.8), kind=kOutput, calls=%fused_computation.10 | convolution fusion | flops 8589934592 | bytes 39845888 | tf_op jit(solution)/shard_map/dot_general | solution.py:72
  250.6 5.7 %copy.20 = f32[4096,256]{1,0:T(8,128)} copy(f32[4096,256]{0,1:T(8,128)} %fusion.14) | data formatting | bytes 8388608 | tf_op jit(solution)/shard_map/dot_general | solution.py:72
  260.4 9.4 %collective-permute-done.36 = f32[64,8,256]{2,1,0:T(8,128)S(1)} collective-permute-done((f32[64,8,256]{2,1,0:T(8,128)S(1)}, f32[64,8,256]{2,1,0:T(8,128)S(1)}, u32[]{:S(2)}, u32[]{:S(2)}) %collective-permute-start.36) | collective-permute-done | bytes 524320 | tf_op jit(solution)/shard_map/ppermute | solution.py:11
  269.7 4.7 %collective-permute-done.37 = f32[64,8,256]{2,1,0:T(8,128)S(1)} collective-permute-done((f32[64,8,256]{2,1,0:T(8,128)S(1)}, f32[64,8,256]{2,1,0:T(8,128)S(1)}, u32[]{:S(2)}, u32[]{:S(2)}) %collective-permute-start.37) | collective-permute-done | bytes 524320 | tf_op jit(solution)/shard_map/ppermute | solution.py:15
  286.9 7.1 %collective-permute-start.40 = (f32[1,48,256]{2,1,0:T(8,128)S(1)}, f32[1,48,256]{2,1,0:T(8,128)S(1)}, u32[]{:S(2)}, u32[]{:S(2)}) collective-permute-start(f32[1,48,256]{2,1,0:T(8,128)S(1)} %get-tuple-element.27), channel_id=1, source_target_pairs={{0,1},{1,2},{2,3},{4,5},{5,6},{6,7}} | collective-permute-start | bytes 147464 | tf_op jit(solution)/shard_map/ppermute | solution.py:11
  322.2 17.4 %fusion.17 = f32[4096,256]{0,1:T(8,128)} fusion(bf16[4096,256]{1,0:T(8,128)(2,1)} %bitcast.48, bf16[1,1,4096,4096]{3,2,1,0:T(8,128)(2,1)} %param.8), kind=kOutput, calls=%fused_computation.11 | convolution fusion | flops 8589934592 | bytes 39845888 | tf_op jit(solution)/shard_map/dot_general | solution.py:72
  339.7 5.7 %copy.21 = f32[4096,256]{1,0:T(8,128)} copy(f32[4096,256]{0,1:T(8,128)} %fusion.17) | data formatting | bytes 8388608 | tf_op jit(solution)/shard_map/dot_general | solution.py:72
  349.4 9.4 %collective-permute-done.48 = f32[64,8,256]{2,1,0:T(8,128)S(1)} collective-permute-done((f32[64,8,256]{2,1,0:T(8,128)S(1)}, f32[64,8,256]{2,1,0:T(8,128)S(1)}, u32[]{:S(2)}, u32[]{:S(2)}) %collective-permute-start.48) | collective-permute-done | bytes 524320 | tf_op jit(solution)/shard_map/ppermute | solution.py:11
  358.8 4.7 %collective-permute-done.49 = f32[64,8,256]{2,1,0:T(8,128)S(1)} collective-permute-done((f32[64,8,256]{2,1,0:T(8,128)S(1)}, f32[64,8,256]{2,1,0:T(8,128)S(1)}, u32[]{:S(2)}, u32[]{:S(2)}) %collective-permute-start.49) | collective-permute-done | bytes 524320 | tf_op jit(solution)/shard_map/ppermute | solution.py:15
  (148 shorter events, 177.9 us)
Async XLA Ops:
  0.7 15.1 %collective-permute-start.1 = (f32[1,48]{1,0:T(1,128)S(1)}, f32[1,48]{1,0:T(1,128)S(1)}, u32[]{:S(2)}, u32[]{:S(2)}) collective-permute-start(f32[1,48]{1,0:T(1,128)S(1)} %get-tuple-element.61), channel_id=1, source_target_pairs={{1,0},{2,1},{3,2},{5,4},{6,5},{7,6}} | collective-permute-start | bytes 584 | tf_op jit(solution)/shard_map/ppermute | solution.py:15
  2.0 15.1 %collective-permute-start = (f32[1,48]{1,0:T(1,128)S(1)}, f32[1,48]{1,0:T(1,128)S(1)}, u32[]{:S(2)}, u32[]{:S(2)}) collective-permute-start(f32[1,48]{1,0:T(1,128)S(1)} %get-tuple-element.62), channel_id=1, source_target_pairs={{0,1},{1,2},{2,3},{4,5},{5,6},{6,7}} | collective-permute-start | bytes 584 | tf_op jit(solution)/shard_map/ppermute | solution.py:11
  6.3 15.3 %collective-permute-start.5 = (f32[48,1]{1,0:T(8,128)S(1)}, f32[48,1]{1,0:T(8,128)S(1)}, u32[]{:S(2)}, u32[]{:S(2)}) collective-permute-start(f32[48,1]{1,0:T(8,128)S(1)} %get-tuple-element.65), channel_id=1, source_target_pairs={{4,0},{5,1},{6,2},{7,3}} | collective-permute-start | bytes 584 | tf_op jit(solution)/shard_map/ppermute | solution.py:15
  7.6 15.3 %collective-permute-start.4 = (f32[48,1]{1,0:T(8,128)S(1)}, f32[48,1]{1,0:T(8,128)S(1)}, u32[]{:S(2)}, u32[]{:S(2)}) collective-permute-start(f32[48,1]{1,0:T(8,128)S(1)} %get-tuple-element.66), channel_id=1, source_target_pairs={{0,4},{1,5},{2,6},{3,7}} | collective-permute-start | bytes 584 | tf_op jit(solution)/shard_map/ppermute | solution.py:11
  13.7 10.2 %collective-permute-start.6 = (f32[48,1,256]{2,1,0:T(1,128)S(1)}, f32[48,1,256]{2,1,0:T(1,128)S(1)}, u32[]{:S(2)}, u32[]{:S(2)}) collective-permute-start(f32[48,1,256]{2,1,0:T(1,128)S(1)} %get-tuple-element.41), channel_id=1, source_target_pairs={{0,4},{1,5},{2,6},{3,7}} | collective-permute-start | bytes 147464 | tf_op jit(solution)/shard_map/ppermute | solution.py:11
  47.4 8.7 %collective-permute-start.11 = (bf16[64,8,256]{2,1,0:T(8,128)(2,1)S(1)}, bf16[64,8,256]{2,1,0:T(8,128)(2,1)S(1)}, u32[]{:S(2)}, u32[]{:S(2)}) collective-permute-start(bf16[64,8,256]{2,1,0:T(8,128)(2,1)S(1)} %get-tuple-element.50), channel_id=1, source_target_pairs={{4,0},{5,1},{6,2},{7,3}} | collective-permute-start | bytes 786440 | tf_op jit(solution)/shard_map/ppermute | solution.py:15
  80.0 12.2 %collective-permute-start.12 = (f32[64,8,256]{2,1,0:T(8,128)S(1)}, f32[64,8,256]{2,1,0:T(8,128)S(1)}, u32[]{:S(2)}, u32[]{:S(2)}) collective-permute-start(f32[64,8,256]{2,1,0:T(8,128)S(1)} %get-tuple-element.17), channel_id=1, source_target_pairs={{0,4},{1,5},{2,6},{3,7}} | collective-permute-start | bytes 1572872 | tf_op jit(solution)/shard_map/ppermute | solution.py:11
  81.5 15.4 %collective-permute-start.13 = (f32[64,8,256]{2,1,0:T(8,128)S(1)}, f32[64,8,256]{2,1,0:T(8,128)S(1)}, u32[]{:S(2)}, u32[]{:S(2)}) collective-permute-start(f32[64,8,256]{2,1,0:T(8,128)S(1)} %get-tuple-element.18), channel_id=1, source_target_pairs={{4,0},{5,1},{6,2},{7,3}} | collective-permute-start | bytes 1572872 | tf_op jit(solution)/shard_map/ppermute | solution.py:15
  106.2 12.1 %collective-permute-start.18 = (f32[48,1,256]{2,1,0:T(1,128)S(1)}, f32[48,1,256]{2,1,0:T(1,128)S(1)}, u32[]{:S(2)}, u32[]{:S(2)}) collective-permute-start(f32[48,1,256]{2,1,0:T(1,128)S(1)} %get-tuple-element.37), channel_id=1, source_target_pairs={{0,4},{1,5},{2,6},{3,7}} | collective-permute-start | bytes 147464 | tf_op jit(solution)/shard_map/ppermute | solution.py:11
  107.9 10.4 %collective-permute-start.19 = (f32[48,1,256]{2,1,0:T(1,128)S(1)}, f32[48,1,256]{2,1,0:T(1,128)S(1)}, u32[]{:S(2)}, u32[]{:S(2)}) collective-permute-start(f32[48,1,256]{2,1,0:T(1,128)S(1)} %get-tuple-element.38), channel_id=1, source_target_pairs={{4,0},{5,1},{6,2},{7,3}} | collective-permute-start | bytes 147464 | tf_op jit(solution)/shard_map/ppermute | solution.py:15
  109.2 9.1 %collective-permute-start.16 = (f32[1,48,256]{2,1,0:T(8,128)S(1)}, f32[1,48,256]{2,1,0:T(8,128)S(1)}, u32[]{:S(2)}, u32[]{:S(2)}) collective-permute-start(f32[1,48,256]{2,1,0:T(8,128)S(1)} %get-tuple-element.35), channel_id=1, source_target_pairs={{0,1},{1,2},{2,3},{4,5},{5,6},{6,7}} | collective-permute-start | bytes 147464 | tf_op jit(solution)/shard_map/ppermute | solution.py:11
  136.8 8.7 %collective-permute-start.23 = (bf16[64,8,256]{2,1,0:T(8,128)(2,1)S(1)}, bf16[64,8,256]{2,1,0:T(8,128)(2,1)S(1)}, u32[]{:S(2)}, u32[]{:S(2)}) collective-permute-start(bf16[64,8,256]{2,1,0:T(8,128)(2,1)S(1)} %get-tuple-element.48), channel_id=1, source_target_pairs={{4,0},{5,1},{6,2},{7,3}} | collective-permute-start | bytes 786440 | tf_op jit(solution)/shard_map/ppermute | solution.py:15
  169.4 12.2 %collective-permute-start.24 = (f32[64,8,256]{2,1,0:T(8,128)S(1)}, f32[64,8,256]{2,1,0:T(8,128)S(1)}, u32[]{:S(2)}, u32[]{:S(2)}) collective-permute-start(f32[64,8,256]{2,1,0:T(8,128)S(1)} %get-tuple-element.15), channel_id=1, source_target_pairs={{0,4},{1,5},{2,6},{3,7}} | collective-permute-start | bytes 1572872 | tf_op jit(solution)/shard_map/ppermute | solution.py:11
  170.9 15.4 %collective-permute-start.25 = (f32[64,8,256]{2,1,0:T(8,128)S(1)}, f32[64,8,256]{2,1,0:T(8,128)S(1)}, u32[]{:S(2)}, u32[]{:S(2)}) collective-permute-start(f32[64,8,256]{2,1,0:T(8,128)S(1)} %get-tuple-element.16), channel_id=1, source_target_pairs={{4,0},{5,1},{6,2},{7,3}} | collective-permute-start | bytes 1572872 | tf_op jit(solution)/shard_map/ppermute | solution.py:15
  195.7 11.6 %collective-permute-start.30 = (f32[48,1,256]{2,1,0:T(1,128)S(1)}, f32[48,1,256]{2,1,0:T(1,128)S(1)}, u32[]{:S(2)}, u32[]{:S(2)}) collective-permute-start(f32[48,1,256]{2,1,0:T(1,128)S(1)} %get-tuple-element.33), channel_id=1, source_target_pairs={{0,4},{1,5},{2,6},{3,7}} | collective-permute-start | bytes 147464 | tf_op jit(solution)/shard_map/ppermute | solution.py:11
  197.6 9.7 %collective-permute-start.31 = (f32[48,1,256]{2,1,0:T(1,128)S(1)}, f32[48,1,256]{2,1,0:T(1,128)S(1)}, u32[]{:S(2)}, u32[]{:S(2)}) collective-permute-start(f32[48,1,256]{2,1,0:T(1,128)S(1)} %get-tuple-element.34), channel_id=1, source_target_pairs={{4,0},{5,1},{6,2},{7,3}} | collective-permute-start | bytes 147464 | tf_op jit(solution)/shard_map/ppermute | solution.py:15
  225.0 8.7 %collective-permute-start.35 = (bf16[64,8,256]{2,1,0:T(8,128)(2,1)S(1)}, bf16[64,8,256]{2,1,0:T(8,128)(2,1)S(1)}, u32[]{:S(2)}, u32[]{:S(2)}) collective-permute-start(bf16[64,8,256]{2,1,0:T(8,128)(2,1)S(1)} %get-tuple-element.46), channel_id=1, source_target_pairs={{4,0},{5,1},{6,2},{7,3}} | collective-permute-start | bytes 786440 | tf_op jit(solution)/shard_map/ppermute | solution.py:15
  257.6 12.2 %collective-permute-start.36 = (f32[64,8,256]{2,1,0:T(8,128)S(1)}, f32[64,8,256]{2,1,0:T(8,128)S(1)}, u32[]{:S(2)}, u32[]{:S(2)}) collective-permute-start(f32[64,8,256]{2,1,0:T(8,128)S(1)} %get-tuple-element.13), channel_id=1, source_target_pairs={{0,4},{1,5},{2,6},{3,7}} | collective-permute-start | bytes 1572872 | tf_op jit(solution)/shard_map/ppermute | solution.py:11
  259.1 15.4 %collective-permute-start.37 = (f32[64,8,256]{2,1,0:T(8,128)S(1)}, f32[64,8,256]{2,1,0:T(8,128)S(1)}, u32[]{:S(2)}, u32[]{:S(2)}) collective-permute-start(f32[64,8,256]{2,1,0:T(8,128)S(1)} %get-tuple-element.14), channel_id=1, source_target_pairs={{4,0},{5,1},{6,2},{7,3}} | collective-permute-start | bytes 1572872 | tf_op jit(solution)/shard_map/ppermute | solution.py:15
  283.9 11.4 %collective-permute-start.42 = (f32[48,1,256]{2,1,0:T(1,128)S(1)}, f32[48,1,256]{2,1,0:T(1,128)S(1)}, u32[]{:S(2)}, u32[]{:S(2)}) collective-permute-start(f32[48,1,256]{2,1,0:T(1,128)S(1)} %get-tuple-element.29), channel_id=1, source_target_pairs={{0,4},{1,5},{2,6},{3,7}} | collective-permute-start | bytes 147464 | tf_op jit(solution)/shard_map/ppermute | solution.py:11
  285.6 9.7 %collective-permute-start.43 = (f32[48,1,256]{2,1,0:T(1,128)S(1)}, f32[48,1,256]{2,1,0:T(1,128)S(1)}, u32[]{:S(2)}, u32[]{:S(2)}) collective-permute-start(f32[48,1,256]{2,1,0:T(1,128)S(1)} %get-tuple-element.30), channel_id=1, source_target_pairs={{4,0},{5,1},{6,2},{7,3}} | collective-permute-start | bytes 147464 | tf_op jit(solution)/shard_map/ppermute | solution.py:15
  312.0 8.7 %collective-permute-start.47 = (bf16[64,8,256]{2,1,0:T(8,128)(2,1)S(1)}, bf16[64,8,256]{2,1,0:T(8,128)(2,1)S(1)}, u32[]{:S(2)}, u32[]{:S(2)}) collective-permute-start(bf16[64,8,256]{2,1,0:T(8,128)(2,1)S(1)} %get-tuple-element.44), channel_id=1, source_target_pairs={{4,0},{5,1},{6,2},{7,3}} | collective-permute-start | bytes 786440 | tf_op jit(solution)/shard_map/ppermute | solution.py:15
  346.6 12.1 %collective-permute-start.48 = (f32[64,8,256]{2,1,0:T(8,128)S(1)}, f32[64,8,256]{2,1,0:T(8,128)S(1)}, u32[]{:S(2)}, u32[]{:S(2)}) collective-permute-start(f32[64,8,256]{2,1,0:T(8,128)S(1)} %get-tuple-element.11), channel_id=1, source_target_pairs={{0,4},{1,5},{2,6},{3,7}} | collective-permute-start | bytes 1572872 | tf_op jit(solution)/shard_map/ppermute | solution.py:11
  348.1 15.4 %collective-permute-start.49 = (f32[64,8,256]{2,1,0:T(8,128)S(1)}, f32[64,8,256]{2,1,0:T(8,128)S(1)}, u32[]{:S(2)}, u32[]{:S(2)}) collective-permute-start(f32[64,8,256]{2,1,0:T(8,128)S(1)} %get-tuple-element.12), channel_id=1, source_target_pairs={{4,0},{5,1},{6,2},{7,3}} | collective-permute-start | bytes 1572872 | tf_op jit(solution)/shard_map/ppermute | solution.py:15
  (35 other events, 245.7 us)
where the time goes:
time: 383 us; the launch traced here: 376 us
  starting transfers between devices  128 us (33%)
  waiting for transfers between devices  109 us (28%)
  matrix products  66.7 us (17%)
  other arithmetic  38.2 us (10%)
  local copies, waits for them, and re-layouts  32.2 us (8%)
    ppermute x26, starting transfers between devices, from_lower(): lax.ppermute(tile_block, axis_name, [(source, source + 1) for source in r...  93.7 us
    dot_general x4, matrix products, local_step(): jnp.dot(matrix, window.reshape(ext_n * ext_n, num_rhs), preferred_element...  66.7 us
    ppermute x26, waiting for transfers between devices, from_upper(): lax.ppermute(tile_block, axis_name, [(source + 1, source) for source in r...  61.2 us
    ppermute x26, waiting for transfers between devices, from_lower(): lax.ppermute(tile_block, axis_name, [(source, source + 1) for source in r...  48.2 us
    ppermute x26, starting transfers between devices, from_upper(): lax.ppermute(tile_block, axis_name, [(source + 1, source) for source in r...  33.8 us
    dot_general x4, local copies, waits for them, and re-layouts, local_step(): jnp.dot(matrix, window.reshape(ext_n * ext_n, num_rhs), preferred_element...  22.8 us
    convert_element_type x4, other arithmetic, local_step(): window = grow_cols(grow_rows(residual.astype(jnp.bfloat16), margin), margin)  20.7 us
    add x4, other arithmetic, fold_cols(): tile_block[:, margin:margin + tile_n]  8.96 us
  transfers between devices with their start and end apart: 52, of which 28 were waited for; matrix products, arithmetic and copies ran while one was open for 1% of the time, Pallas kernels for 0%

commit v1 on v0

v1 whole, which is shorter than its diff:
```python
import functools

import jax
import jax.numpy as jnp
from jax import lax
from jax.experimental import pallas as pl
from jax.experimental.pallas import tpu as pltpu
from jax.sharding import PartitionSpec as P

SWEEPS = 4
TILE = 48
EXT = 64
WIN = EXT * EXT
RHS = 256
SIDES = (0, 1)
F32 = jnp.float32
BF16 = jnp.bfloat16
MESH = pl.DeviceIdType.MESH

CHUNKS = ((16, 16, 0), (32, 16, 18), (7, 9, 36), (TILE, 9, 47))
YLEN = 58
RCHUNKS = ((5, 14), (0, 5), (19, 5))


def kernel(omega, f_hbm, u_hbm, kap_hbm, m_hbm, out_hbm,
           ms, mr, w, z, r, u, wx, wy, kown, krecv, kfull,
           ys, yr, xrs, xrr, rsy, rry, rsx, rrx, rrd, ues, uer,
           yz_s, yz_r, xs_s, xs_r, xr_s, xr_r, ry_s, ry_r, rx_s, rx_r, rd_s, rd_r,
           ie_s, ie_r, lsem, msem):
    col = lax.axis_index("col")
    row = lax.axis_index("row")
    has_up = row > 0
    has_dn = row < 3
    ydev = (1 - col, row)
    xdev = ((col, row - 1), (col, row + 1))
    ddev = ((1 - col, row - 1), (1 - col, row + 1))
    has = (has_up, has_dn)

    hc = pl.multiple_of(56 - 56 * col, 8)
    mc = pl.multiple_of(TILE - 40 * col, 8)
    oc = pl.multiple_of(56 * col, 8)
    sc = pl.multiple_of(TILE - TILE * col, 16)
    rc = pl.multiple_of(16 * col, 16)
    gc = pl.multiple_of(8 + 8 * col, 8)
    cd = pl.multiple_of(40 - 32 * col, 8)
    ci = pl.multiple_of(8 + 16 * col, 8)
    es = 55 - 47 * col
    er = 56 - 49 * col

    def remote(src, dst, ss, rs, dev):
        return pltpu.make_async_remote_copy(src_ref=src, dst_ref=dst, send_sem=ss, recv_sem=rs,
                                            device_id=dev, device_id_type=MESH)

    inner = (pl.ds(8, TILE), pl.ds(8, TILE))
    cp_k = pltpu.make_async_copy(kap_hbm, kown, lsem.at[0])
    cp_z = pltpu.make_async_copy(u_hbm, z.at[inner], lsem.at[1])
    cp_r = pltpu.make_async_copy(f_hbm, r.at[inner], lsem.at[2])
    cp_u = pltpu.make_async_copy(u_hbm, u, lsem.at[3])
    for cp in (cp_k, cp_z, cp_r):
        cp.start()

    def load_s(i):
        return pltpu.make_async_copy(m_hbm.at[pl.ds(16 * i, 16), pl.ds(sc, 16)], ms.at[pl.ds(16 * i, 16)], msem.at[i])

    def load_r(i):
        return pltpu.make_async_copy(m_hbm.at[pl.ds(16 * i, 16), pl.ds(rc, TILE)], mr.at[pl.ds(16 * i, 16)], msem.at[4 + i])

    for i in range(4):
        load_s(i).start()
    for i in range(4):
        load_r(i).start()
    cp_u.start()

    for ref in (z, r):
        ref[0:8] = jnp.zeros((8, EXT, RHS), F32)
        ref[56:EXT] = jnp.zeros((8, EXT, RHS), F32)
        ref[8:56, 0:8] = jnp.zeros((TILE, 8, RHS), F32)
        ref[8:56, 56:EXT] = jnp.zeros((TILE, 8, RHS), F32)
    kfull[...] = jnp.zeros_like(kfull)
    ys[...] = jnp.zeros_like(ys)

    bar = pltpu.get_barrier_semaphore()
    pl.semaphore_signal(bar, inc=1, device_id=ydev, device_id_type=MESH)
    for d in SIDES:
        @pl.when(has[d])
        def _(d=d):
            pl.semaphore_signal(bar, inc=1, device_id=xdev[d], device_id_type=MESH)
            pl.semaphore_signal(bar, inc=1, device_id=ddev[d], device_id_type=MESH)
    n_sides = has_up.astype(jnp.int32) + has_dn.astype(jnp.int32)
    pl.semaphore_wait(bar, 1 + 2 * n_sides)

    cp_k.wait()
    k_y = remote(kown, krecv.at[2], ie_s.at[0], ie_r.at[0], ydev)
    k_y.start()
    k_x = [remote(kown, krecv.at[1 - d], ie_s.at[1 + d], ie_r.at[2 - d], xdev[d]) for d in SIDES]
    u_x = [remote(z.at[8 if d == 0 else 55, pl.ds(8, TILE)], z.at[56 if d == 0 else 7, pl.ds(8, TILE)],
                  ie_s.at[3 + d], ie_r.at[4 - d], xdev[d]) for d in SIDES]
    k_in = [remote(kown, krecv.at[d], ie_s.at[1 + d], ie_r.at[1 + d], xdev[d]) for d in SIDES]
    u_in = [remote(z.at[8 if d == 0 else 55, pl.ds(8, TILE)], z.at[7 if d == 0 else 56, pl.ds(8, TILE)],
                   ie_s.at[3 + d], ie_r.at[3 + d], xdev[d]) for d in SIDES]
    cp_z.wait()
    for k in range(TILE):
        ues[k // 8, k % 8, :] = z[8 + k, pl.ds(es, 1), :][0]
    u_y = remote(ues, uer, ie_s.at[5], ie_r.at[5], ydev)
    u_y.start()
    for d in SIDES:
        @pl.when(has[d])
        def _(d=d):
            k_x[d].start()
            u_x[d].start()

    kfull[8:56, 8:56] = kown[...]
    for d in SIDES:
        @pl.when(has[d])
        def _(d=d):
            k_in[d].wait_recv()
            src = 47 if d == 0 else 0
            dst = 7 if d == 0 else 56
            kfull[dst:dst + 1, 8:56] = krecv[d, src:src + 1, :]
    k_y.wait_recv()

    @pl.when(col == 0)
    def _():
        kfull[8:56, 56:57] = krecv[2, :, 0:1]

    @pl.when(col == 1)
    def _():
        kfull[8:56, 7:8] = krecv[2, :, 47:TILE]

    kt = kfull[...].T
    prev = jnp.broadcast_to(kt[0:EXT, 7:8], (EXT, 128))
    for a in range(8, 57):
        here = jnp.broadcast_to(kt[0:EXT, a:a + 1], (EXT, 128))
        wx[a - 8] = 0.5 * (prev + here)
        if a < 56:
            wy[a - 8] = 0.5 * (pltpu.roll(here, 1, 0) + here)
        prev = here

    def both(v):
        return jnp.concatenate([v, v], axis=1)

    def update(a0, rows, c0, n, om, add_u):
        def body(i, carry):
            a = a0 + i
            wide = z[a, pl.ds(c0 - 8, n + 16), :]
            fy = both(wy[a - 8, pl.ds(c0 - 8, n + 16), :]) * (wide - pltpu.roll(wide, 1, 0))
            fyr = pltpu.roll(fy, n + 15, 0)
            mid = wide[8:8 + n]
            az = (both(wx[a - 8, pl.ds(c0, n), :]) * (mid - z[a - 1, pl.ds(c0, n), :])
                  + both(wx[a - 7, pl.ds(c0, n), :]) * (mid - z[a + 1, pl.ds(c0, n), :])
                  + fy[8:8 + n] - fyr[8:8 + n])
            r[a, pl.ds(c0, n), :] = r[a, pl.ds(c0, n), :] - om * az
            if add_u:
                u[a - 8, pl.ds(c0 - 8, n), :] = u[a - 8, pl.ds(c0 - 8, n), :] + om * mid
            return carry
        lax.fori_loop(0, rows, body, 0)

    def ry(j):
        p0, n = RCHUNKS[j]
        return remote(rsy.at[pl.ds(p0, n)], rry.at[pl.ds(p0, n)], ry_s.at[j], ry_r.at[j], ydev)

    def rx(d):
        return remote(rsx.at[d], rrx.at[1 - d], rx_s.at[d], rx_r.at[1 - d], xdev[d])

    def rx_in(d):
        return remote(rsx.at[d], rrx.at[d], rx_s.at[d], rx_r.at[d], xdev[d])

    def rd(d):
        return remote(rsy.at[pl.ds(20 * d, 4)], rrd.at[1 - d], rd_s.at[d], rd_r.at[1 - d], ddev[d])

    def rd_in(d):
        return remote(rsy.at[pl.ds(20 * d, 4)], rrd.at[d], rd_s.at[d], rd_r.at[d], ddev[d])

    def send_ry(j):
        p0, n = RCHUNKS[j]
        for p in range(p0, p0 + n):
            a = 8 + 2 * p
            rsy[p] = jnp.concatenate([r[a, pl.ds(mc, 8), :], r[a + 1, pl.ds(mc, 8), :]], axis=0).astype(BF16)
        ry(j).start()

    def send_rx():
        for d in SIDES:
            for i in range(8):
                rsx[d, i] = r[8 + 40 * d + i, 8:56, :].astype(BF16)

            @pl.when(has[d])
            def _(d=d):
                rd(d).start()
                rx(d).start()

    def to_w(a0, rows, c0, n):
        def body(i, carry):
            w[a0 + i, pl.ds(c0, n), :] = r[a0 + i, pl.ds(c0, n), :].astype(BF16)
            return carry
        lax.fori_loop(0, rows, body, 0)

    def recv_r():
        to_w(8, TILE, rc, TILE)
        for d in SIDES:
            @pl.when(has[d])
            def _(d=d):
                rx_in(d).wait_recv()
                rd_in(d).wait_recv()
                for i in range(8):
                    r[56 * d + i, 8:56, :] = rrx[d, i].astype(F32)
                for q in range(4):
                    v = rrd[d, q].astype(F32)
                    r[56 * d + 2 * q, pl.ds(hc, 8), :] = v[0:8]
                    r[56 * d + 2 * q + 1, pl.ds(hc, 8), :] = v[8:16]
            to_w(56 * d, 8, 0, EXT)
        for j in range(3):
            p0, n = RCHUNKS[j]
            ry(j).wait_recv()

            def body(i, carry, p0=p0):
                v = rry[p0 + i].astype(F32)
                a = 8 + 2 * (p0 + i)
                r[a, pl.ds(hc, 8), :] = v[0:8]
                r[a + 1, pl.ds(hc, 8), :] = v[8:16]
                w[a, pl.ds(sc, 16), :] = r[a, pl.ds(sc, 16), :].astype(BF16)
                w[a + 1, pl.ds(sc, 16), :] = r[a + 1, pl.ds(sc, 16), :].astype(BF16)
                return carry
            lax.fori_loop(0, n, body, 0)
        for j in range(3):
            ry(j).wait_send()
        for d in SIDES:
            @pl.when(has[d])
            def _(d=d):
                rx(d).wait_send()
                rd(d).wait_send()

    for d in SIDES:
        @pl.when(has[d])
        def _(d=d):
            u_in[d].wait_recv()
    u_y.wait_recv()
    for k in range(TILE):
        z[8 + k, pl.ds(er, 1), :] = uer[k // 8, k % 8, :][None]
    cp_r.wait()
    update(8, TILE, cd, 16, 1.0, False)
    for j in range(3):
        send_ry(j)
    update(8, TILE, ci, 32, 1.0, False)
    send_rx()
    recv_r()
    k_y.wait_send()
    u_y.wait_send()
    for d in SIDES:
        @pl.when(has[d])
        def _(d=d):
            k_x[d].wait_send()
            u_x[d].wait_send()
    cp_u.wait()

    om = omega[0]

    def dot_s(a0):
        lhs = ms[pl.ds(a0, 16)].reshape(RHS, WIN)
        z[pl.ds(a0, 16), pl.ds(sc, 16), :] = jnp.dot(
            lhs, w[...].reshape(WIN, RHS), preferred_element_type=F32).reshape(16, 16, RHS)

    def dot_r(a0):
        lhs = mr[pl.ds(a0, 16)].reshape(768, WIN)
        z[pl.ds(a0, 16), pl.ds(rc, TILE), :] = jnp.dot(
            lhs, w[...].reshape(WIN, RHS), preferred_element_type=F32).reshape(16, TILE, RHS)

    def yz(j):
        a0, n, off = CHUNKS[j]
        length = n + 2
        return remote(ys.at[pl.ds(off, length)], yr.at[pl.ds(off, length)], yz_s.at[j], yz_r.at[j], ydev)

    def send_y(j):
        a0, n, off = CHUNKS[j]
        for k in range(n):
            ys[off + k] = z[a0 + k, pl.ds(hc, 8), :]
            ys[off + n + k // 8, k % 8, :] = z[a0 + k, pl.ds(es, 1), :][0]
        yz(j).start()

    def recv_y(j):
        a0, n, off = CHUNKS[j]
        yz(j).wait_recv()
        for k in range(n):
            z[a0 + k, pl.ds(mc, 8), :] = z[a0 + k, pl.ds(mc, 8), :] + yr[off + k]
            z[a0 + k, pl.ds(er, 1), :] = z[a0 + k, pl.ds(er, 1), :] + yr[off + n + k // 8, k % 8, :][None]

    def xs(d):
        return remote(z.at[pl.ds(55 * d, 9), pl.ds(sc, 16)], xrs.at[1 - d], xs_s.at[d], xs_r.at[1 - d], xdev[d])

    def xs_in(d):
        return remote(z.at[pl.ds(55 * d, 9), pl.ds(sc, 16)], xrs.at[d], xs_s.at[d], xs_r.at[d], xdev[d])

    def xr(d):
        return remote(z.at[pl.ds(55 * d, 9), pl.ds(gc, 40)], xrr.at[1 - d], xr_s.at[d], xr_r.at[1 - d], xdev[d])

    def xr_in(d):
        return remote(z.at[pl.ds(55 * d, 9), pl.ds(gc, 40)], xrr.at[d], xr_s.at[d], xr_r.at[d], xdev[d])

    def on_side(d, fn):
        pl.when(has[d])(fn)

    def sweep(s, carry):
        @pl.when(s == 0)
        def _():
            for i in range(4):
                load_s(i).wait()
        dot_s(16)
        send_y(0)
        dot_s(32)
        send_y(1)
        lax.fori_loop(0, 2, lambda i, c: (dot_s(TILE * i), c)[1], 0)
        for d in SIDES:
            on_side(d, lambda d=d: xs(d).start())

            @pl.when(jnp.logical_not(has[d]))
            def _(d=d):
                z[7 + 49 * d, pl.ds(sc, 16), :] = jnp.zeros((16, RHS), F32)

        @pl.when(s == 0)
        def _():
            for i in range(4):
                load_r(i).wait()
        lax.fori_loop(0, 2, lambda i, c: (dot_r(TILE * i), c)[1], 0)
        for d in SIDES:
            on_side(d, lambda d=d: xr(d).start())
        for d in SIDES:
            @pl.when(has[d])
            def _(d=d):
                xs(d).wait_send()
                xs_in(d).wait_recv()
                a0 = 7 + 41 * d
                for k in range(9):
                    z[a0 + k, pl.ds(sc, 16), :] = z[a0 + k, pl.ds(sc, 16), :] + xrs[d, k]
            send_y(2 + d)
        lax.fori_loop(1, 3, lambda i, c: (dot_r(16 * i), c)[1], 0)
        for d in SIDES:
            @pl.when(jnp.logical_not(has[d]))
            def _(d=d):
                z[7 + 49 * d, :, :] = jnp.zeros((EXT, RHS), F32)
        z[:, pl.ds(oc, 8), :] = jnp.zeros((EXT, 8, RHS), F32)
        recv_y(0)
        recv_y(1)

        @pl.when(s < SWEEPS - 1)
        def _():
            update(17, 30, cd, 16, om, True)
            send_ry(0)
            update(17, 30, ci, 32, om, True)
        for d in SIDES:
            @pl.when(has[d])
            def _(d=d):
                xr(d).wait_send()
                xr_in(d).wait_recv()
                a0 = 7 + 41 * d
                for k in range(9):
                    z[a0 + k, pl.ds(gc, 40), :] = z[a0 + k, pl.ds(gc, 40), :] + xrr[d, k]
        recv_y(2)
        recv_y(3)

        @pl.when(s < SWEEPS - 1)
        def _():
            lax.fori_loop(0, 2, lambda i, c: (update(8 + 39 * i, 9, cd, 16, om, True), c)[1], 0)
            send_ry(1)
            send_ry(2)
            lax.fori_loop(0, 2, lambda i, c: (update(8 + 39 * i, 9, ci, 32, om, True), c)[1], 0)
            send_rx()
            recv_r()

        @pl.when(s == SWEEPS - 1)
        def _():
            def body(i, c):
                u[i] = u[i] + om * z[8 + i, 8:56, :]
                return c
            lax.fori_loop(0, TILE, body, 0)
        for j in range(4):
            yz(j).wait_send()
        return carry

    lax.fori_loop(0, SWEEPS, sweep, 0)
    cp_o = pltpu.make_async_copy(u, out_hbm, lsem.at[4])
    cp_o.start()
    cp_o.wait()


def solution(mesh):
    def local_step(forcing, u_init, diffusivity, local_solve, relax_omega):
        any_spec = pl.BlockSpec(memory_space=pl.ANY)
        dma = pltpu.SemaphoreType.DMA
        return pl.pallas_call(
            kernel,
            out_shape=jax.ShapeDtypeStruct((TILE, TILE, RHS), F32),
            in_specs=[pl.BlockSpec(memory_space=pltpu.SMEM)] + [any_spec] * 4,
            out_specs=any_spec,
            scratch_shapes=[
                pltpu.VMEM((EXT, 16, WIN), BF16),
                pltpu.VMEM((EXT, TILE, WIN), BF16),
                pltpu.VMEM((EXT, EXT, RHS), BF16),
                pltpu.VMEM((EXT, EXT, RHS), F32),
                pltpu.VMEM((EXT, EXT, RHS), F32),
                pltpu.VMEM((TILE, TILE, RHS), F32),
                pltpu.VMEM((49, EXT, 128), F32),
                pltpu.VMEM((TILE, EXT, 128), F32),
                pltpu.VMEM((TILE, TILE), F32),
                pltpu.VMEM((3, TILE, TILE), F32),
                pltpu.VMEM((128, 128), F32),
                pltpu.VMEM((YLEN, 8, RHS), F32),
                pltpu.VMEM((YLEN, 8, RHS), F32),
                pltpu.VMEM((2, 9, 16, RHS), F32),
                pltpu.VMEM((2, 9, 40, RHS), F32),
                pltpu.VMEM((24, 16, RHS), BF16),
                pltpu.VMEM((24, 16, RHS), BF16),
                pltpu.VMEM((2, 8, TILE, RHS), BF16),
                pltpu.VMEM((2, 8, TILE, RHS), BF16),
                pltpu.VMEM((2, 4, 16, RHS), BF16),
                pltpu.VMEM((6, 8, RHS), F32),
                pltpu.VMEM((6, 8, RHS), F32),
                dma((4,)), dma((4,)), dma((2,)), dma((2,)), dma((2,)), dma((2,)),
                dma((3,)), dma((3,)), dma((2,)), dma((2,)), dma((2,)), dma((2,)),
                dma((6,)), dma((6,)), dma((5,)), dma((8,)),
            ],
            compiler_params=pltpu.CompilerParams(
                collective_id=0, has_side_effects=True, vmem_limit_bytes=64_000_000),
            name="schwarz",
        )(relax_omega.reshape(1), forcing, u_init, diffusivity,
          local_solve.reshape(EXT, EXT, WIN))

    field_spec = P('row', 'col', None)
    return jax.shard_map(local_step, mesh=mesh,
                         in_specs=(field_spec, field_spec, P('row', 'col'), P('row', 'col', None, None), P()),
                         out_specs=field_spec, check_vma=False)
```

time: 383 us -> 98.5 us (0.26); the launches traced: 376 us -> 98 us
  starting transfers between devices: 128 us -> 0 us
  waiting for transfers between devices: 109 us -> 0 us
  Pallas kernels: 0 us -> 94.1 us
  matrix products: 66.7 us -> 0 us
  other arithmetic: 38.2 us -> 0 us
  local copies, waits for them, and re-layouts: 32.2 us -> 3.23 us
    ppermute x52 -> x0, starting transfers between devices: 128 us -> none  [the longest x26 93.7 us: from_lower(): lax.ppermute(tile_block, axis_name, [(source, source + 1) for source in r...]
    ppermute x52 -> x0, waiting for transfers between devices: 109 us -> none  [the longest x26 61.2 us: from_upper(): lax.ppermute(tile_block, axis_name, [(source + 1, source) for source in r...]
    pallas_call x0 -> x1, Pallas kernels: none -> 94.1 us  [local_step(): pl.pallas_call(kernel, out_shape=jax.ShapeDtypeStruct((TILE, TILE, RHS),...]
    dot_general x4 -> x0, matrix products: 66.7 us -> none  [local_step(): jnp.dot(matrix, window.reshape(ext_n * ext_n, num_rhs), preferred_element...]
    dot_general x4 -> x0, local copies, waits for them, and re-layouts: 22.8 us -> none  [local_step(): jnp.dot(matrix, window.reshape(ext_n * ext_n, num_rhs), preferred_element...]
    convert_element_type x4 -> x0, other arithmetic: 20.7 us -> none  [local_step(): window = grow_cols(grow_rows(residual.astype(jnp.bfloat16), margin), margin)]
    add x8 -> x0, other arithmetic: 12.5 us -> none  [the longest x4 8.96 us: fold_cols(): tile_block[:, margin:margin + tile_n]]
    slice x24 -> x0, local copies, waits for them, and re-layouts: 9.35 us -> none  [the longest x4 5.09 us: fold_cols(): from_left = from_lower(tile_block[:, margin + tile_n:], 'col', cols_dev)]
  transfers between devices with their start and end apart: 52 -> 0, of which waited for: 28 -> 0; matrix products, arithmetic and copies ran while one was open for 1% -> 0% of each run, Pallas kernels for 0% -> 0%
where the time goes in v1:
time: 98.5 us; the launch traced here: 98 us
  Pallas kernels  94.1 us (96%)
  local copies, waits for them, and re-layouts  3.23 us (3%)
    pallas_call x1, Pallas kernels, local_step(): pl.pallas_call(kernel, out_shape=jax.ShapeDtypeStruct((TILE, TILE, RHS),...  94.1 us
    unnamed x1, local copies, waits for them, and re-layouts  3.23 us

profile of v1, /device:TPU:0, one launch (start us, length us, event | category | flops | bytes accessed | tf_op | source)
XLA Modules:
  0.0 98.0 jit_solution(17037037292727215792)
XLA Ops:
  0.7 94.1 %schwarz.1 = f32[48,48,256]{2,1,0:T(8,128)} custom-call(f32[1]{0:T(128)} %bitcast.2.omega, f32[48,48,256]{2,1,0:T(8,128)} %f_hbm.1, f32[48,48,256]{2,1,0:T(8,128)} %u_hbm.1, f32[48,48]{1,0:T(8,128)} %kap_hbm.1, bf16[64,64,4096]{2,1,0:T(8,128)(2,1)} %bitcast.3), custom_call_target="tpu_custom_call" | custom-call | tf_op jit(solution)/shard_map/schwarz/pallas_call | solution.py:388
  94.8 3.2 %copy.8 = f32[48,48,256]{2,1,0:T(8,128)} copy(f32[48,48,256]{2,1,0:T(8,128)} %schwarz.1) | data formatting | bytes 4718592

commit v2 on v1

v2 whole, which is shorter than its diff:
```python
import functools

import jax
import jax.numpy as jnp
from jax import lax
from jax.experimental import pallas as pl
from jax.experimental.pallas import tpu as pltpu
from jax.sharding import PartitionSpec as P

SWEEPS = 4
TILE = 48
EXT = 64
WIN = EXT * EXT
RHS = 256
MG = 8
STRIP = 16
REST = 40
END = 56
SIDES = (0, 1)
F32 = jnp.float32
BF16 = jnp.bfloat16
MESH = pl.DeviceIdType.MESH

CHUNKS = ((STRIP, 12, 0), (36, 12, 14), (28, MG, 28))
SIDE_OFF = 37
YLEN = 59
RMID = (9, 6)
FCHUNKS = ((4, MG), (12, MG))

def kernel(omega, f_hbm, u_hbm, kap_hbm, m_hbm, u,
           ms, mr, w, z, r, wx, wy, kown, krecv, kfull,
           ys, yr, xrs, xrr, rsy, rry, rsx, rrx, rrd, ues, uer,
           fys, fyr_, fxs, fxsr, fxr, fxrr,
           yz_s, yz_r, xs_s, xs_r, xr_s, xr_r, ry_s, ry_r, rx_s, rx_r, rd_s, rd_r,
           ie_s, ie_r, fy_s, fy_r, fx_s, fx_r, lsem, msem):
    col = lax.axis_index("col")
    row = lax.axis_index("row")
    has_up = row > 0
    has_dn = row < 3
    ydev = (1 - col, row)
    has = (has_up, has_dn)
    first = jnp.where(row < 2, 1, 0)
    order = (first, 1 - first)

    def xdev(d):
        return (col, row - 1 + 2 * d)

    def ddev(d):
        return (1 - col, row - 1 + 2 * d)

    def on_side(d, fn):
        there = jnp.where(d == 0, row, 3 - row) > 0
        pl.when(there)(fn)

    def off_side(d, fn):
        there = jnp.where(d == 0, row, 3 - row) > 0
        pl.when(jnp.logical_not(there))(fn)

    hc = pl.multiple_of(END - END * col, MG)
    mc = pl.multiple_of(TILE - REST * col, MG)
    oc = pl.multiple_of(END * col, MG)
    sc = pl.multiple_of(TILE - TILE * col, STRIP)
    rc = pl.multiple_of(STRIP * col, STRIP)
    gc = pl.multiple_of(MG + MG * col, MG)
    cd = pl.multiple_of(REST - 32 * col, MG)
    ci = pl.multiple_of(MG + STRIP * col, MG)
    es = 55 - 47 * col
    er = END - 49 * col

    def remote(src, dst, ss, rs, dev):
        return pltpu.make_async_remote_copy(src_ref=src, dst_ref=dst, send_sem=ss, recv_sem=rs,
                                            device_id=dev, device_id_type=MESH)

    inner = (pl.ds(MG, TILE), pl.ds(MG, TILE))
    cp_k = pltpu.make_async_copy(kap_hbm, kown, lsem.at[0])
    cp_z = pltpu.make_async_copy(u_hbm, z.at[inner], lsem.at[1])
    cp_r = pltpu.make_async_copy(f_hbm, r.at[inner], lsem.at[2])
    cp_u = pltpu.make_async_copy(u_hbm, u, lsem.at[3])
    for cp in (cp_k, cp_z, cp_r):
        cp.start()

    def load_s(i):
        return pltpu.make_async_copy(m_hbm.at[pl.ds(STRIP * i, STRIP), pl.ds(sc, STRIP)], ms.at[pl.ds(STRIP * i, STRIP)], msem.at[i])

    def load_r(i):
        return pltpu.make_async_copy(m_hbm.at[pl.ds(STRIP * i, STRIP), pl.ds(gc, REST)], mr.at[pl.ds(STRIP * i, STRIP)], msem.at[4 + i])

    for i in range(4):
        load_s(i).start()
    for i in range(4):
        load_r(i).start()
    cp_u.start()

    for ref in (z, r):
        ref[0:MG] = jnp.zeros((MG, EXT, RHS), F32)
        ref[END:EXT] = jnp.zeros((MG, EXT, RHS), F32)
        ref[MG:END, 0:MG] = jnp.zeros((TILE, MG, RHS), F32)
        ref[MG:END, END:EXT] = jnp.zeros((TILE, MG, RHS), F32)
    kfull[...] = jnp.zeros_like(kfull)
    ys[...] = jnp.zeros_like(ys)

    bar = pltpu.get_barrier_semaphore()
    pl.semaphore_signal(bar, inc=1, device_id=ydev, device_id_type=MESH)
    for d in SIDES:
        @pl.when(has[d])
        def _(d=d):
            pl.semaphore_signal(bar, inc=1, device_id=xdev(d), device_id_type=MESH)
            pl.semaphore_signal(bar, inc=1, device_id=ddev(d), device_id_type=MESH)
    n_sides = has_up.astype(jnp.int32) + has_dn.astype(jnp.int32)
    pl.semaphore_wait(bar, 1 + 2 * n_sides)

    cp_k.wait()
    k_y = remote(kown, krecv.at[2], ie_s.at[0], ie_r.at[0], ydev)
    k_y.start()
    k_x = [remote(kown, krecv.at[1 - d], ie_s.at[1 + d], ie_r.at[2 - d], xdev(d)) for d in SIDES]
    u_x = [remote(z.at[MG if d == 0 else 55, pl.ds(MG, TILE)], z.at[END if d == 0 else 7, pl.ds(MG, TILE)],
                  ie_s.at[3 + d], ie_r.at[4 - d], xdev(d)) for d in SIDES]
    k_in = [remote(kown, krecv.at[d], ie_s.at[1 + d], ie_r.at[1 + d], xdev(d)) for d in SIDES]
    u_in = [remote(z.at[MG if d == 0 else 55, pl.ds(MG, TILE)], z.at[7 if d == 0 else END, pl.ds(MG, TILE)],
                   ie_s.at[3 + d], ie_r.at[3 + d], xdev(d)) for d in SIDES]
    cp_z.wait()
    for k in range(TILE):
        ues[k // MG, k % MG, :] = z[MG + k, pl.ds(es, 1), :][0]
    u_y = remote(ues, uer, ie_s.at[5], ie_r.at[5], ydev)
    u_y.start()
    for d in SIDES:
        @pl.when(has[d])
        def _(d=d):
            k_x[d].start()
            u_x[d].start()

    kfull[MG:END, MG:END] = kown[...]
    for d in SIDES:
        @pl.when(has[d])
        def _(d=d):
            k_in[d].wait_recv()
            src = 47 if d == 0 else 0
            dst = 7 if d == 0 else END
            kfull[dst:dst + 1, MG:END] = krecv[d, src:src + 1, :]
    k_y.wait_recv()

    @pl.when(col == 0)
    def _():
        kfull[MG:END, END:57] = krecv[2, :, 0:1]

    @pl.when(col == 1)
    def _():
        kfull[MG:END, 7:MG] = krecv[2, :, 47:TILE]

    kt = kfull[...].T
    prev = jnp.broadcast_to(kt[0:EXT, 7:MG], (EXT, 128))
    for a in range(MG, 57):
        here = jnp.broadcast_to(kt[0:EXT, a:a + 1], (EXT, 128))
        wx[a - MG] = 0.5 * (prev + here)
        if a < END:
            wy[a - MG] = 0.5 * (pltpu.roll(here, 1, 0) + here)
        prev = here

    def both(v):
        return jnp.concatenate([v, v], axis=1)

    def update(a0, rows, c0, n, om, add_u):
        def body(i, carry):
            a = a0 + i
            wide = z[a, pl.ds(c0 - MG, n + STRIP), :]
            fy = both(wy[a - MG, pl.ds(c0 - MG, n + STRIP), :]) * (wide - pltpu.roll(wide, 1, 0))
            fyr = pltpu.roll(fy, n + 15, 0)
            mid = wide[MG:MG + n]
            az = (both(wx[a - MG, pl.ds(c0, n), :]) * (mid - z[a - 1, pl.ds(c0, n), :])
                  + both(wx[a - 7, pl.ds(c0, n), :]) * (mid - z[a + 1, pl.ds(c0, n), :])
                  + fy[MG:MG + n] - fyr[MG:MG + n])
            r[a, pl.ds(c0, n), :] = r[a, pl.ds(c0, n), :] - om * az
            if add_u:
                u[a - MG, pl.ds(c0 - MG, n), :] = u[a - MG, pl.ds(c0 - MG, n), :] + om * mid
            return carry
        lax.fori_loop(0, rows, body, 0)

    def ry(p0, n, j):
        return remote(rsy.at[pl.ds(p0, n)], rry.at[pl.ds(p0, n)], ry_s.at[j], ry_r.at[j], ydev)

    def ry_mid():
        return ry(*RMID, 2)

    def ry_side(d):
        return ry(15 * d, 9, d)

    def rx(d):
        return remote(rsx.at[d], rrx.at[1 - d], rx_s.at[d], rx_r.at[1 - d], xdev(d))

    def rx_in(d):
        return remote(rsx.at[d], rrx.at[d], rx_s.at[d], rx_r.at[d], xdev(d))

    def rd(d):
        return remote(rsy.at[pl.ds(20 * d, 4)], rrd.at[1 - d], rd_s.at[d], rd_r.at[1 - d], ddev(d))

    def rd_in(d):
        return remote(rsy.at[pl.ds(20 * d, 4)], rrd.at[d], rd_s.at[d], rd_r.at[d], ddev(d))

    def pack_ry(p0, n):
        for q in range(n):
            a = MG + 2 * (p0 + q)
            rsy[p0 + q] = jnp.concatenate([r[a, pl.ds(mc, MG), :], r[a + 1, pl.ds(mc, MG), :]], axis=0).astype(BF16)

    def send_ry_side(d):
        pack_ry(15 * d, 9)
        on_side(d, lambda: rd(d).start())
        ry_side(d).start()

    def send_ry_mid():
        pack_ry(*RMID)
        ry_mid().start()

    def send_rx(d):
        for i in range(MG):
            rsx[d, i] = r[MG + REST * d + i, MG:END, :].astype(BF16)
        on_side(d, lambda: rx(d).start())

    def to_w(a0, rows, c0, n):
        def body(i, carry):
            w[a0 + i, pl.ds(c0, n), :] = r[a0 + i, pl.ds(c0, n), :].astype(BF16)
            return carry
        lax.fori_loop(0, rows, body, 0)

    def unpack_ry(p0, n):
        def body(i, carry):
            v = rry[p0 + i].astype(F32)
            a = MG + 2 * (p0 + i)
            r[a, pl.ds(hc, MG), :] = v[0:MG]
            r[a + 1, pl.ds(hc, MG), :] = v[MG:STRIP]
            w[a, pl.ds(sc, STRIP), :] = r[a, pl.ds(sc, STRIP), :].astype(BF16)
            w[a + 1, pl.ds(sc, STRIP), :] = r[a + 1, pl.ds(sc, STRIP), :].astype(BF16)
            return carry
        lax.fori_loop(0, n, body, 0)

    def recv_r():
        to_w(MG, TILE, rc, TILE)
        for d in (order[1], order[0]):
            ry_side(d).wait_recv()
            unpack_ry(15 * d, 9)

            def side(d=d):
                rx_in(d).wait_recv()
                rd_in(d).wait_recv()
                for i in range(MG):
                    r[END * d + i, MG:END, :] = rrx[d, i].astype(F32)
                for q in range(4):
                    v = rrd[d, q].astype(F32)
                    r[END * d + 2 * q, pl.ds(hc, MG), :] = v[0:MG]
                    r[END * d + 2 * q + 1, pl.ds(hc, MG), :] = v[MG:STRIP]
                to_w(END * d, MG, 0, EXT)
            on_side(d, side)
        ry_mid().wait_recv()
        unpack_ry(*RMID)
        ry_mid().wait_send()
        for d in SIDES:
            ry_side(d).wait_send()

            def sent(d=d):
                rx(d).wait_send()
                rd(d).wait_send()
            on_side(d, sent)

    for d in SIDES:
        @pl.when(has[d])
        def _(d=d):
            u_in[d].wait_recv()
    u_y.wait_recv()
    for k in range(TILE):
        z[MG + k, pl.ds(er, 1), :] = uer[k // MG, k % MG, :][None]
    cp_r.wait()
    update(MG, TILE, cd, STRIP, 1.0, False)
    for d in SIDES:
        send_ry_side(d)
    send_ry_mid()
    update(MG, TILE, ci, 32, 1.0, False)
    for d in SIDES:
        send_rx(d)
        off_side(d, lambda d=d: to_w(END * d, MG, 0, EXT))
    recv_r()
    k_y.wait_send()
    u_y.wait_send()
    for d in SIDES:
        @pl.when(has[d])
        def _(d=d):
            k_x[d].wait_send()
            u_x[d].wait_send()
    cp_u.wait()

    om = omega[0]

    def dot_s(a0):
        lhs = ms[pl.ds(a0, STRIP)].reshape(RHS, WIN)
        z[pl.ds(a0, STRIP), pl.ds(sc, STRIP), :] = jnp.dot(
            lhs, w[...].reshape(WIN, RHS), preferred_element_type=F32).reshape(STRIP, STRIP, RHS)

    def dot_r(a0):
        lhs = mr[pl.ds(a0, STRIP)].reshape(640, WIN)
        z[pl.ds(a0, STRIP), pl.ds(gc, REST), :] = jnp.dot(
            lhs, w[...].reshape(WIN, RHS), preferred_element_type=F32).reshape(STRIP, REST, RHS)

    def yz(j, off, length):
        return remote(ys.at[pl.ds(off, length)], yr.at[pl.ds(off, length)], yz_s.at[j], yz_r.at[j], ydev)

    def yz_mid(j):
        return yz(j, CHUNKS[j][2], CHUNKS[j][1] + pl.cdiv(CHUNKS[j][1], MG))

    def yz_side(d):
        return yz(3 + d, SIDE_OFF + 11 * d, 11)

    def pack_y(a0, n, off):
        for k in range(n):
            ys[off + k] = z[a0 + k, pl.ds(hc, MG), :]
            ys[off + n + k // MG, k % MG, :] = z[a0 + k, pl.ds(es, 1), :][0]

    def add_y(a0, n, off):
        for k in range(n):
            z[a0 + k, pl.ds(mc, MG), :] = z[a0 + k, pl.ds(mc, MG), :] + yr[off + k]
            z[a0 + k, pl.ds(er, 1), :] = z[a0 + k, pl.ds(er, 1), :] + yr[off + n + k // MG, k % MG, :][None]

    def send_y(j):
        pack_y(*CHUNKS[j])
        yz_mid(j).start()

    def send_y_side(d):
        pack_y(7 + 41 * d, 9, SIDE_OFF + 11 * d)
        yz_side(d).start()

    def recv_y(j):
        yz_mid(j).wait_recv()
        add_y(*CHUNKS[j])

    def recv_y_side(d):
        yz_side(d).wait_recv()
        add_y(7 + 41 * d, 9, SIDE_OFF + 11 * d)

    def xs(d):
        return remote(z.at[pl.ds(55 * d, 9), pl.ds(sc, STRIP)], xrs.at[1 - d], xs_s.at[d], xs_r.at[1 - d], xdev(d))

    def xs_in(d):
        return remote(z.at[pl.ds(55 * d, 9), pl.ds(sc, STRIP)], xrs.at[d], xs_s.at[d], xs_r.at[d], xdev(d))

    def xr(d):
        return remote(z.at[pl.ds(55 * d, 9), pl.ds(gc, REST)], xrr.at[1 - d], xr_s.at[d], xr_r.at[1 - d], xdev(d))

    def xr_in(d):
        return remote(z.at[pl.ds(55 * d, 9), pl.ds(gc, REST)], xrr.at[d], xr_s.at[d], xr_r.at[d], xdev(d))

    def fold_s(d):
        def side():
            xs(d).wait_send()
            xs_in(d).wait_recv()
            for k in range(9):
                a = 7 + 41 * d + k
                z[a, pl.ds(sc, STRIP), :] = z[a, pl.ds(sc, STRIP), :] + xrs[d, k]
        on_side(d, side)

    def fold_r(d):
        def side():
            xr(d).wait_send()
            xr_in(d).wait_recv()
            for k in range(9):
                a = 7 + 41 * d + k
                z[a, pl.ds(gc, REST), :] = z[a, pl.ds(gc, REST), :] + xrr[d, k]
        on_side(d, side)

    def no_row_s(d):
        z[7 + 49 * d, pl.ds(sc, STRIP), :] = jnp.zeros((STRIP, RHS), F32)

    def no_row_r(d):
        z[7 + 49 * d, pl.ds(gc, REST), :] = jnp.zeros((REST, RHS), F32)

    def sweep(s, carry):
        @pl.when(s == 0)
        def _():
            for i in range(4):
                load_s(i).wait()
        dot_s(STRIP)
        send_y(0)
        dot_s(32)
        send_y(1)
        for d in order:
            dot_s(TILE * d)
            on_side(d, lambda d=d: xs(d).start())
            off_side(d, lambda d=d: no_row_s(d))

        @pl.when(s == 0)
        def _():
            for i in range(4):
                load_r(i).wait()
        for d in order:
            dot_r(TILE * d)
            on_side(d, lambda d=d: xr(d).start())
            off_side(d, lambda d=d: no_row_r(d))
            fold_s(1 - d)
            send_y_side(1 - d)
        send_y(2)
        dot_r(STRIP)
        dot_r(32)
        recv_y(0)
        recv_y(1)
        for d in (order[1], order[0]):
            fold_r(d)
            update(MG + 39 * d, 9, ci, 32, om, True)
            recv_y_side(d)
            update(MG + 30 * d, 18, cd, STRIP, om, True)
            send_ry_side(d)
            send_rx(d)
        update(17, 30, ci, 32, om, True)
        recv_y(2)
        update(26, 12, cd, STRIP, om, True)
        send_ry_mid()
        recv_r()
        for j in range(3):
            yz_mid(j).wait_send()
        for d in SIDES:
            yz_side(d).wait_send()
        return carry

    lax.fori_loop(0, SWEEPS - 1, sweep, 0)

    def fy(j, p0, n):
        return remote(fys.at[pl.ds(p0, n)], fyr_.at[pl.ds(p0, n)], fy_s.at[j], fy_r.at[j], ydev)

    def send_fy(j, p0, n):
        for q in range(n):
            a = MG + 2 * (p0 + q)
            fys[p0 + q] = jnp.concatenate([z[a, pl.ds(hc, MG), :], z[a + 1, pl.ds(hc, MG), :]], axis=0).astype(BF16)
        fy(j, p0, n).start()

    def fxsd(d):
        return remote(fxs.at[d], fxsr.at[1 - d], fx_s.at[d], fx_r.at[1 - d], xdev(d))

    def fxsd_in(d):
        return remote(fxs.at[d], fxsr.at[d], fx_s.at[d], fx_r.at[d], xdev(d))

    def fxrd(d):
        return remote(fxr.at[d], fxrr.at[1 - d], fx_s.at[2 + d], fx_r.at[3 - d], xdev(d))

    def fxrd_in(d):
        return remote(fxr.at[d], fxrr.at[d], fx_s.at[2 + d], fx_r.at[2 + d], xdev(d))

    def last_s(d):
        for i in range(MG):
            fxs[d, i] = z[END * d + i, pl.ds(sc, STRIP), :].astype(BF16)
        fxsd(d).start()

    def last_r(d):
        for i in range(4):
            a = END * d + 2 * i
            fxr[d, i] = jnp.concatenate([z[a, pl.ds(gc, REST), :], z[a + 1, pl.ds(gc, REST), :]], axis=0).astype(BF16)
        fxrd(d).start()

    def last_fold_s(d):
        fxsd_in(d).wait_recv()
        for i in range(MG):
            a = MG + REST * d + i
            z[a, pl.ds(sc, STRIP), :] = z[a, pl.ds(sc, STRIP), :] + fxsr[d, i].astype(F32)

    def last_fold_r(d):
        fxrd_in(d).wait_recv()
        for i in range(4):
            a = MG + REST * d + 2 * i
            v = fxrr[d, i].astype(F32)
            z[a, pl.ds(gc, REST), :] = z[a, pl.ds(gc, REST), :] + v[0:REST]
            z[a + 1, pl.ds(gc, REST), :] = z[a + 1, pl.ds(gc, REST), :] + v[REST:80]

    def last_y(j, p0, n):
        fy(j, p0, n).wait_recv()

        def body(i, c):
            v = fyr_[p0 + i].astype(F32)
            a = MG + 2 * (p0 + i)
            z[a, pl.ds(mc, MG), :] = z[a, pl.ds(mc, MG), :] + v[0:MG]
            z[a + 1, pl.ds(mc, MG), :] = z[a + 1, pl.ds(mc, MG), :] + v[MG:STRIP]
            return c
        lax.fori_loop(0, n, body, 0)

    def add_u(a0, rows):
        def body(i, c):
            u[a0 - MG + i] = u[a0 - MG + i] + om * z[a0 + i, MG:END, :]
            return c
        lax.fori_loop(0, rows, body, 0)

    for j in SIDES:
        dot_s(STRIP + STRIP * j)
        send_fy(j, *FCHUNKS[j])
    for d in order:
        dot_s(TILE * d)
        on_side(d, lambda d=d: last_s(d))
    for d in order:
        dot_r(TILE * d)
        on_side(d, lambda d=d: last_r(d))
        on_side(1 - d, lambda d=d: last_fold_s(1 - d))
        send_fy(3 - d, 20 * (1 - d), 4)
    dot_r(STRIP)
    dot_r(32)
    for j in SIDES:
        last_y(j, *FCHUNKS[j])
    add_u(STRIP, 32)
    for d in (order[1], order[0]):
        on_side(d, lambda d=d: last_fold_r(d))
        last_y(2 + d, 20 * d, 4)
        add_u(MG + REST * d, MG)
    for j in SIDES:
        fy(j, *FCHUNKS[j]).wait_send()
        fy(2 + j, 20 * j, 4).wait_send()

        def sent(j=j):
            fxsd(j).wait_send()
            fxrd(j).wait_send()
        on_side(j, sent)


def solution(mesh):
    def local_step(forcing, u_init, diffusivity, local_solve, relax_omega):
        any_spec = pl.BlockSpec(memory_space=pltpu.HBM)
        dma = pltpu.SemaphoreType.DMA
        return pl.pallas_call(
            kernel,
            out_shape=jax.ShapeDtypeStruct((TILE, TILE, RHS), F32),
            in_specs=[pl.BlockSpec(memory_space=pltpu.SMEM)] + [any_spec] * 4,
            out_specs=pl.BlockSpec(memory_space=pltpu.VMEM),
            scratch_shapes=[
                pltpu.VMEM((EXT, STRIP, WIN), BF16),
                pltpu.VMEM((EXT, REST, WIN), BF16),
                pltpu.VMEM((EXT, EXT, RHS), BF16),
                pltpu.VMEM((EXT, EXT, RHS), F32),
                pltpu.VMEM((EXT, EXT, RHS), F32),
                pltpu.VMEM((49, EXT, 128), F32),
                pltpu.VMEM((TILE, EXT, 128), F32),
                pltpu.VMEM((TILE, TILE), F32),
                pltpu.VMEM((3, TILE, TILE), F32),
                pltpu.VMEM((128, 128), F32),
                pltpu.VMEM((YLEN, MG, RHS), F32),
                pltpu.VMEM((YLEN, MG, RHS), F32),
                pltpu.VMEM((2, 9, STRIP, RHS), F32),
                pltpu.VMEM((2, 9, REST, RHS), F32),
                pltpu.VMEM((24, STRIP, RHS), BF16),
                pltpu.VMEM((24, STRIP, RHS), BF16),
                pltpu.VMEM((2, MG, TILE, RHS), BF16),
                pltpu.VMEM((2, MG, TILE, RHS), BF16),
                pltpu.VMEM((2, 4, STRIP, RHS), BF16),
                pltpu.VMEM((6, MG, RHS), F32),
                pltpu.VMEM((6, MG, RHS), F32),
                pltpu.VMEM((24, STRIP, RHS), BF16),
                pltpu.VMEM((24, STRIP, RHS), BF16),
                pltpu.VMEM((2, MG, STRIP, RHS), BF16),
                pltpu.VMEM((2, MG, STRIP, RHS), BF16),
                pltpu.VMEM((2, 4, 80, RHS), BF16),
                pltpu.VMEM((2, 4, 80, RHS), BF16),
                dma((5,)), dma((5,)), dma((2,)), dma((2,)), dma((2,)), dma((2,)),
                dma((3,)), dma((3,)), dma((2,)), dma((2,)), dma((2,)), dma((2,)),
                dma((6,)), dma((6,)), dma((4,)), dma((4,)), dma((4,)), dma((4,)), dma((4,)), dma((MG,)),
            ],
            compiler_params=pltpu.CompilerParams(
                collective_id=0, has_side_effects=True, vmem_limit_bytes=54_000_000),
            name="schwarz",
        )(relax_omega.reshape(1), forcing, u_init, diffusivity,
          local_solve.reshape(EXT, EXT, WIN))

    field_spec = P('row', 'col', None)
    return jax.shard_map(local_step, mesh=mesh,
                         in_specs=(field_spec, field_spec, P('row', 'col'), P('row', 'col', None, None), P()),
                         out_specs=field_spec, check_vma=False)
```

time: 98.5 us -> 102 us (1.036)
  Pallas kernels: 94.1 us -> 98.6 us
  local copies, waits for them, and re-layouts: 3.23 us -> 2.14 us
    pallas_call x1, Pallas kernels: 94.1 us -> 98.6 us  [local_step(): pl.pallas_call(kernel, out_shape=jax.ShapeDtypeStruct((TILE, TILE, RHS),...]
    unnamed x1 -> x3, local copies, waits for them, and re-layouts: 3.23 us -> 2.14 us
where the time goes in v2:
time: 102 us; the launch traced here: 101 us
  Pallas kernels  98.6 us (97%)
  local copies, waits for them, and re-layouts  2.14 us (2%)
    pallas_call x1, Pallas kernels, local_step(): pl.pallas_call(kernel, out_shape=jax.ShapeDtypeStruct((TILE, TILE, RHS),...  98.6 us
    unnamed x3, local copies, waits for them, and re-layouts  2.14 us

profile of v2, /device:TPU:0, one launch (start us, length us, event | category | flops | bytes accessed | tf_op | source)
XLA Modules:
  0.0 101.4 jit_solution(17873244346319813587)
XLA Ops:
  0.7 0.0 copy-start
  0.7 0.7 copy-done
  1.4 98.6 %schwarz.1 = f32[48,48,256]{2,1,0:T(8,128)S(1)} custom-call(f32[1]{0:T(128)} %bitcast.2.omega, f32[48,48,256]{2,1,0:T(8,128)} %f_hbm.1, f32[48,48,256]{2,1,0:T(8,128)} %u_hbm.1, f32[48,48]{1,0:T(8,128)S(1)} %copy-done, bf16[64,64,4096]{2,1,0:T(8,128)(2,1)} %bitcast.3), custom_call_target="tpu_custom_call" | custom-call | tf_op jit(solution)/shard_map/schwarz/pallas_call | solution.py:518
  100.0 1.4 %copy.8 = f32[48,48,256]{2,1,0:T(8,128)} copy(f32[48,48,256]{2,1,0:T(8,128)S(1)} %schwarz.1) | data formatting | bytes 4718592
Async XLA Ops:
  0.7 0.7 copy-start

commit v3 on v2

--- a/solution.py
+++ b/solution.py
@@ -378,33 +378,42 @@
         send_y(0)
         dot_s(32)
         send_y(1)
-        for d in order:
+
+        def ends_s(i, c):
+            d = jnp.where(i == 0, first, 1 - first)
             dot_s(TILE * d)
-            on_side(d, lambda d=d: xs(d).start())
-            off_side(d, lambda d=d: no_row_s(d))
+            on_side(d, lambda: xs(d).start())
+            off_side(d, lambda: no_row_s(d))
+            return c
+        lax.fori_loop(0, 2, ends_s, 0)
 
         @pl.when(s == 0)
         def _():
             for i in range(4):
                 load_r(i).wait()
-        for d in order:
+        def ends_r(i, c):
+            d = jnp.where(i == 0, first, 1 - first)
             dot_r(TILE * d)
-            on_side(d, lambda d=d: xr(d).start())
-            off_side(d, lambda d=d: no_row_r(d))
+            on_side(d, lambda: xr(d).start())
+            off_side(d, lambda: no_row_r(d))
             fold_s(1 - d)
             send_y_side(1 - d)
+            return c
+        lax.fori_loop(0, 2, ends_r, 0)
         send_y(2)
-        dot_r(STRIP)
-        dot_r(32)
+        lax.fori_loop(1, 3, lambda i, c: (dot_r(STRIP * i), c)[1], 0)
         recv_y(0)
         recv_y(1)
-        for d in (order[1], order[0]):
+        def ends_u(i, c):
+            d = jnp.where(i == 0, 1 - first, first)
             fold_r(d)
             update(MG + 39 * d, 9, ci, 32, om, True)
             recv_y_side(d)
             update(MG + 30 * d, 18, cd, STRIP, om, True)
             send_ry_side(d)
             send_rx(d)
+            return c
+        lax.fori_loop(0, 2, ends_u, 0)
         update(17, 30, ci, 32, om, True)
         recv_y(2)
         update(26, 12, cd, STRIP, om, True)
@@ -484,16 +493,23 @@
     for j in SIDES:
         dot_s(STRIP + STRIP * j)
         send_fy(j, *FCHUNKS[j])
-    for d in order:
+
+    def last_ends_s(i, c):
+        d = jnp.where(i == 0, first, 1 - first)
         dot_s(TILE * d)
-        on_side(d, lambda d=d: last_s(d))
-    for d in order:
+        on_side(d, lambda: last_s(d))
+        return c
+    lax.fori_loop(0, 2, last_ends_s, 0)
+
+    def last_ends_r(i, c):
+        d = jnp.where(i == 0, first, 1 - first)
         dot_r(TILE * d)
-        on_side(d, lambda d=d: last_r(d))
-        on_side(1 - d, lambda d=d: last_fold_s(1 - d))
+        on_side(d, lambda: last_r(d))
+        on_side(1 - d, lambda: last_fold_s(1 - d))
         send_fy(3 - d, 20 * (1 - d), 4)
-    dot_r(STRIP)
-    dot_r(32)
+        return c
+    lax.fori_loop(0, 2, last_ends_r, 0)
+    lax.fori_loop(1, 3, lambda i, c: (dot_r(STRIP * i), c)[1], 0)
     for j in SIDES:
         last_y(j, *FCHUNKS[j])
     add_u(STRIP, 32)

time: 102 us -> 89.7 us (0.88)
  Pallas kernels: 98.6 us -> 86.7 us
    pallas_call x1, Pallas kernels: 98.6 us -> 86.7 us  [local_step(): pl.pallas_call(kernel, out_shape=jax.ShapeDtypeStruct((TILE, TILE, RHS),...]
where the time goes in v3:
time: 89.7 us; the launch traced here: 89.5 us
  Pallas kernels  86.7 us (97%)
  local copies, waits for them, and re-layouts  2.14 us (2%)
    pallas_call x1, Pallas kernels, local_step(): pl.pallas_call(kernel, out_shape=jax.ShapeDtypeStruct((TILE, TILE, RHS),...  86.7 us
    unnamed x3, local copies, waits for them, and re-layouts  2.14 us

profile of v3, /device:TPU:0, one launch (start us, length us, event | category | flops | bytes accessed | tf_op | source)
XLA Modules:
  0.0 89.5 jit_solution(8233655069525840227)
XLA Ops:
  0.7 0.0 copy-start
  0.7 0.7 copy-done
  1.4 86.7 %schwarz.1 = f32[48,48,256]{2,1,0:T(8,128)S(1)} custom-call(f32[1]{0:T(128)} %bitcast.2.omega, f32[48,48,256]{2,1,0:T(8,128)} %f_hbm.1, f32[48,48,256]{2,1,0:T(8,128)} %u_hbm.1, f32[48,48]{1,0:T(8,128)S(1)} %copy-done, bf16[64,64,4096]{2,1,0:T(8,128)(2,1)} %bitcast.3), custom_call_target="tpu_custom_call" | custom-call | tf_op jit(solution)/shard_map/schwarz/pallas_call | solution.py:534
  88.1 1.4 %copy.8 = f32[48,48,256]{2,1,0:T(8,128)} copy(f32[48,48,256]{2,1,0:T(8,128)S(1)} %schwarz.1) | data formatting | bytes 4718592
Async XLA Ops:
  0.7 0.7 copy-start

commit v4 on v3

--- a/solution.py
+++ b/solution.py
@@ -85,12 +85,6 @@
     def load_r(i):
         return pltpu.make_async_copy(m_hbm.at[pl.ds(STRIP * i, STRIP), pl.ds(gc, REST)], mr.at[pl.ds(STRIP * i, STRIP)], msem.at[4 + i])
 
-    for i in range(4):
-        load_s(i).start()
-    for i in range(4):
-        load_r(i).start()
-    cp_u.start()
-
     for ref in (z, r):
         ref[0:MG] = jnp.zeros((MG, EXT, RHS), F32)
         ref[END:EXT] = jnp.zeros((MG, EXT, RHS), F32)
@@ -118,16 +112,21 @@
     k_in = [remote(kown, krecv.at[d], ie_s.at[1 + d], ie_r.at[1 + d], xdev(d)) for d in SIDES]
     u_in = [remote(z.at[MG if d == 0 else 55, pl.ds(MG, TILE)], z.at[7 if d == 0 else END, pl.ds(MG, TILE)],
                    ie_s.at[3 + d], ie_r.at[3 + d], xdev(d)) for d in SIDES]
+    for d in SIDES:
+        on_side(d, lambda d=d: k_x[d].start())
     cp_z.wait()
     for k in range(TILE):
         ues[k // MG, k % MG, :] = z[MG + k, pl.ds(es, 1), :][0]
     u_y = remote(ues, uer, ie_s.at[5], ie_r.at[5], ydev)
     u_y.start()
     for d in SIDES:
-        @pl.when(has[d])
-        def _(d=d):
-            k_x[d].start()
-            u_x[d].start()
+        on_side(d, lambda d=d: u_x[d].start())
+    cp_r.wait()
+    for i in range(4):
+        load_s(i).start()
+    for i in range(4):
+        load_r(i).start()
+    cp_u.start()
 
     kfull[MG:END, MG:END] = kown[...]
     for d in SIDES:
@@ -267,15 +266,18 @@
     u_y.wait_recv()
     for k in range(TILE):
         z[MG + k, pl.ds(er, 1), :] = uer[k // MG, k % MG, :][None]
-    cp_r.wait()
-    update(MG, TILE, cd, STRIP, 1.0, False)
+    update(MG, 18, cd, STRIP, 1.0, False)
+    update(38, 18, cd, STRIP, 1.0, False)
     for d in SIDES:
         send_ry_side(d)
+    update(26, 12, cd, STRIP, 1.0, False)
     send_ry_mid()
-    update(MG, TILE, ci, 32, 1.0, False)
+    update(MG, MG, ci, 32, 1.0, False)
+    update(TILE, MG, ci, 32, 1.0, False)
     for d in SIDES:
         send_rx(d)
         off_side(d, lambda d=d: to_w(END * d, MG, 0, EXT))
+    update(STRIP, 32, ci, 32, 1.0, False)
     recv_r()
     k_y.wait_send()
     u_y.wait_send()

time: 89.7 us -> 85.6 us (0.954)
  Pallas kernels: 86.7 us -> 82.6 us
    pallas_call x1, Pallas kernels: 86.7 us -> 82.6 us  [local_step(): pl.pallas_call(kernel, out_shape=jax.ShapeDtypeStruct((TILE, TILE, RHS),...]
where the time goes in v4:
time: 85.6 us; the launch traced here: 85.4 us
  Pallas kernels  82.6 us (96%)
  local copies, waits for them, and re-layouts  2.14 us (2%)
    pallas_call x1, Pallas kernels, local_step(): pl.pallas_call(kernel, out_shape=jax.ShapeDtypeStruct((TILE, TILE, RHS),...  82.6 us
    unnamed x3, local copies, waits for them, and re-layouts  2.14 us

profile of v4, /device:TPU:0, one launch (start us, length us, event | category | flops | bytes accessed | tf_op | source)
XLA Modules:
  0.0 85.4 jit_solution(17828866958599497649)
XLA Ops:
  0.7 0.0 copy-start
  0.7 0.7 copy-done
  1.4 82.6 %schwarz.1 = f32[48,48,256]{2,1,0:T(8,128)S(1)} custom-call(f32[1]{0:T(128)} %bitcast.2.omega, f32[48,48,256]{2,1,0:T(8,128)} %f_hbm.1, f32[48,48,256]{2,1,0:T(8,128)} %u_hbm.1, f32[48,48]{1,0:T(8,128)S(1)} %copy-done, bf16[64,64,4096]{2,1,0:T(8,128)(2,1)} %bitcast.3), custom_call_target="tpu_custom_call" | custom-call | tf_op jit(solution)/shard_map/schwarz/pallas_call | solution.py:536
  84.0 1.4 %copy.8 = f32[48,48,256]{2,1,0:T(8,128)} copy(f32[48,48,256]{2,1,0:T(8,128)S(1)} %schwarz.1) | data formatting | bytes 4718592
Async XLA Ops:
  0.7 0.7 copy-start

commit v5 on v4

--- a/solution.py
+++ b/solution.py
@@ -21,10 +21,11 @@
 BF16 = jnp.bfloat16
 MESH = pl.DeviceIdType.MESH
 
-CHUNKS = ((STRIP, 12, 0), (36, 12, 14), (28, MG, 28))
-SIDE_OFF = 37
-YLEN = 59
-RMID = (9, 6)
+CHUNKS = ((16, 16, 0), (40, 8, 18), (32, 8, 27))
+SIDE_OFF = 36
+YLEN = 56
+RMID = (11, 6)
+REARLY = (7, 4)
 FCHUNKS = ((4, MG), (12, MG))
 
 def kernel(omega, f_hbm, u_hbm, kap_hbm, m_hbm, u,
@@ -180,8 +181,11 @@
     def ry_mid():
         return ry(*RMID, 2)
 
+    def ry_early():
+        return ry(*REARLY, 3)
+
     def ry_side(d):
-        return ry(15 * d, 9, d)
+        return ry(17 * d, 7, d)
 
     def rx(d):
         return remote(rsx.at[d], rrx.at[1 - d], rx_s.at[d], rx_r.at[1 - d], xdev(d))
@@ -191,6 +195,12 @@
 
     def rd(d):
         return remote(rsy.at[pl.ds(20 * d, 4)], rrd.at[1 - d], rd_s.at[d], rd_r.at[1 - d], ddev(d))
+
+    def rd_forward(d):
+        return remote(rry.at[pl.ds(20 * d, 4)], rrd.at[1 - d], rd_s.at[d], rd_r.at[1 - d], xdev(d))
+
+    def same_chip(d):
+        return lax.rem(row + d, 2) == 1
 
     def rd_in(d):
         return remote(rsy.at[pl.ds(20 * d, 4)], rrd.at[d], rd_s.at[d], rd_r.at[d], ddev(d))
@@ -201,13 +211,17 @@
             rsy[p0 + q] = jnp.concatenate([r[a, pl.ds(mc, MG), :], r[a + 1, pl.ds(mc, MG), :]], axis=0).astype(BF16)
 
     def send_ry_side(d):
-        pack_ry(15 * d, 9)
-        on_side(d, lambda: rd(d).start())
+        pack_ry(17 * d, 7)
+        on_side(d, lambda: pl.when(jnp.logical_not(same_chip(d)))(lambda: rd(d).start()))
         ry_side(d).start()
 
     def send_ry_mid():
         pack_ry(*RMID)
         ry_mid().start()
+
+    def send_ry_early():
+        pack_ry(*REARLY)
+        ry_early().start()
 
     def send_rx(d):
         for i in range(MG):
@@ -233,10 +247,13 @@
 
     def recv_r():
         to_w(MG, TILE, rc, TILE)
+        ry_early().wait_recv()
+        unpack_ry(*REARLY)
         for d in (order[1], order[0]):
             ry_side(d).wait_recv()
-            unpack_ry(15 * d, 9)
-
+            on_side(d, lambda d=d: pl.when(same_chip(d))(lambda: rd_forward(d).start()))
+            unpack_ry(17 * d, 7)
+        for d in (order[1], order[0]):
             def side(d=d):
                 rx_in(d).wait_recv()
                 rd_in(d).wait_recv()
@@ -251,6 +268,7 @@
         ry_mid().wait_recv()
         unpack_ry(*RMID)
         ry_mid().wait_send()
+        ry_early().wait_send()
         for d in SIDES:
             ry_side(d).wait_send()
 
@@ -266,11 +284,12 @@
     u_y.wait_recv()
     for k in range(TILE):
         z[MG + k, pl.ds(er, 1), :] = uer[k // MG, k % MG, :][None]
-    update(MG, 18, cd, STRIP, 1.0, False)
-    update(38, 18, cd, STRIP, 1.0, False)
+    for d in SIDES:
+        update(MG + 34 * d, 14, cd, STRIP, 1.0, False)
     for d in SIDES:
         send_ry_side(d)
-    update(26, 12, cd, STRIP, 1.0, False)
+    update(22, 20, cd, STRIP, 1.0, False)
+    send_ry_early()
     send_ry_mid()
     update(MG, MG, ci, 32, 1.0, False)
     update(TILE, MG, ci, 32, 1.0, False)
@@ -307,33 +326,38 @@
         return yz(j, CHUNKS[j][2], CHUNKS[j][1] + pl.cdiv(CHUNKS[j][1], MG))
 
     def yz_side(d):
-        return yz(3 + d, SIDE_OFF + 11 * d, 11)
-
-    def pack_y(a0, n, off):
+        return yz(3 + d, SIDE_OFF + 10 * d, 10)
+
+    def pack_y(a0, n, off, e0, ne):
         for k in range(n):
             ys[off + k] = z[a0 + k, pl.ds(hc, MG), :]
-            ys[off + n + k // MG, k % MG, :] = z[a0 + k, pl.ds(es, 1), :][0]
-
-    def add_y(a0, n, off):
+        for k in range(ne):
+            ys[off + n + k // MG, k % MG, :] = z[e0 + k, pl.ds(es, 1), :][0]
+
+    def add_y(a0, n, off, e0, ne):
         for k in range(n):
             z[a0 + k, pl.ds(mc, MG), :] = z[a0 + k, pl.ds(mc, MG), :] + yr[off + k]
-            z[a0 + k, pl.ds(er, 1), :] = z[a0 + k, pl.ds(er, 1), :] + yr[off + n + k // MG, k % MG, :][None]
+        for k in range(ne):
+            z[e0 + k, pl.ds(er, 1), :] = z[e0 + k, pl.ds(er, 1), :] + yr[off + n + k // MG, k % MG, :][None]
+
+    def side_rows(d):
+        return 7 + 41 * d, 9, SIDE_OFF + 10 * d, MG + REST * d, MG
 
     def send_y(j):
-        pack_y(*CHUNKS[j])
+        pack_y(*CHUNKS[j], *CHUNKS[j][:2])
         yz_mid(j).start()
 
     def send_y_side(d):
-        pack_y(7 + 41 * d, 9, SIDE_OFF + 11 * d)
+        pack_y(*side_rows(d))
         yz_side(d).start()
 
     def recv_y(j):
         yz_mid(j).wait_recv()
-        add_y(*CHUNKS[j])
+        add_y(*CHUNKS[j], *CHUNKS[j][:2])
 
     def recv_y_side(d):
         yz_side(d).wait_recv()
-        add_y(7 + 41 * d, 9, SIDE_OFF + 11 * d)
+        add_y(*side_rows(d))
 
     def xs(d):
         return remote(z.at[pl.ds(55 * d, 9), pl.ds(sc, STRIP)], xrs.at[1 - d], xs_s.at[d], xs_r.at[1 - d], xdev(d))
@@ -405,20 +429,23 @@
         send_y(2)
         lax.fori_loop(1, 3, lambda i, c: (dot_r(STRIP * i), c)[1], 0)
         recv_y(0)
+        update(22, MG, cd, STRIP, om, True)
+        send_ry_early()
         recv_y(1)
+
         def ends_u(i, c):
             d = jnp.where(i == 0, 1 - first, first)
             fold_r(d)
             update(MG + 39 * d, 9, ci, 32, om, True)
             recv_y_side(d)
-            update(MG + 30 * d, 18, cd, STRIP, om, True)
+            update(MG + 34 * d, 14, cd, STRIP, om, True)
             send_ry_side(d)
             send_rx(d)
             return c
         lax.fori_loop(0, 2, ends_u, 0)
         update(17, 30, ci, 32, om, True)
         recv_y(2)
-        update(26, 12, cd, STRIP, om, True)
+        update(30, 12, cd, STRIP, om, True)
         send_ry_mid()
         recv_r()
         for j in range(3):
@@ -567,7 +594,7 @@
                 pltpu.VMEM((2, 4, 80, RHS), BF16),
                 pltpu.VMEM((2, 4, 80, RHS), BF16),
                 dma((5,)), dma((5,)), dma((2,)), dma((2,)), dma((2,)), dma((2,)),
-                dma((3,)), dma((3,)), dma((2,)), dma((2,)), dma((2,)), dma((2,)),
+                dma((4,)), dma((4,)), dma((2,)), dma((2,)), dma((2,)), dma((2,)),
                 dma((6,)), dma((6,)), dma((4,)), dma((4,)), dma((4,)), dma((4,)), dma((4,)), dma((MG,)),
             ],
             compiler_params=pltpu.CompilerParams(

time: 85.6 us -> 83.8 us (0.979)
  Pallas kernels: 82.6 us -> 80.9 us
    pallas_call x1, Pallas kernels: 82.6 us -> 80.9 us  [local_step(): pl.pallas_call(kernel, out_shape=jax.ShapeDtypeStruct((TILE, TILE, RHS),...]
where the time goes in v5:
time: 83.8 us; the launch traced here: 83.7 us
  Pallas kernels  80.9 us (97%)
  local copies, waits for them, and re-layouts  2.14 us (3%)
    pallas_call x1, Pallas kernels, local_step(): pl.pallas_call(kernel, out_shape=jax.ShapeDtypeStruct((TILE, TILE, RHS),...  80.9 us
    unnamed x3, local copies, waits for them, and re-layouts  2.14 us

profile of v5, /device:TPU:0, one launch (start us, length us, event | category | flops | bytes accessed | tf_op | source)
XLA Modules:
  0.0 83.7 jit_solution(1873145000887966332)
XLA Ops:
  0.7 0.0 copy-start
  0.7 0.7 copy-done
  1.4 80.9 %schwarz.1 = f32[48,48,256]{2,1,0:T(8,128)S(1)} custom-call(f32[1]{0:T(128)} %bitcast.2.omega, f32[48,48,256]{2,1,0:T(8,128)} %f_hbm.1, f32[48,48,256]{2,1,0:T(8,128)} %u_hbm.1, f32[48,48]{1,0:T(8,128)S(1)} %copy-done, bf16[64,64,4096]{2,1,0:T(8,128)(2,1)} %bitcast.3), custom_call_target="tpu_custom_call" | custom-call | tf_op jit(solution)/shard_map/schwarz/pallas_call | solution.py:563
  82.3 1.4 %copy.8 = f32[48,48,256]{2,1,0:T(8,128)} copy(f32[48,48,256]{2,1,0:T(8,128)S(1)} %schwarz.1) | data formatting | bytes 4718592
Async XLA Ops:
  0.7 0.7 copy-start

commit v6 on v5

--- a/solution.py
+++ b/solution.py
@@ -28,9 +28,9 @@
 REARLY = (7, 4)
 FCHUNKS = ((4, MG), (12, MG))
 
-def kernel(omega, f_hbm, u_hbm, kap_hbm, m_hbm, u,
-           ms, mr, w, z, r, wx, wy, kown, krecv, kfull,
-           ys, yr, xrs, xrr, rsy, rry, rsx, rrx, rrd, ues, uer,
+def kernel(omega, f_hbm, u_hbm, kown, m_hbm, u,
+           ms, mr, w, z, r, wx, wy, krecv, kfull,
+           ys, yr, xrs, xrr, rsy, rry, rsx, rrx, rrd, rdb, ues, uer, pcs, pcr,
            fys, fyr_, fxs, fxsr, fxr, fxrr,
            yz_s, yz_r, xs_s, xs_r, xr_s, xr_r, ry_s, ry_r, rx_s, rx_r, rd_s, rd_r,
            ie_s, ie_r, fy_s, fy_r, fx_s, fx_r, lsem, msem):
@@ -67,17 +67,17 @@
     ci = pl.multiple_of(MG + STRIP * col, MG)
     es = 55 - 47 * col
     er = END - 49 * col
+    face = END - TILE * col
 
     def remote(src, dst, ss, rs, dev):
         return pltpu.make_async_remote_copy(src_ref=src, dst_ref=dst, send_sem=ss, recv_sem=rs,
                                             device_id=dev, device_id_type=MESH)
 
     inner = (pl.ds(MG, TILE), pl.ds(MG, TILE))
-    cp_k = pltpu.make_async_copy(kap_hbm, kown, lsem.at[0])
     cp_z = pltpu.make_async_copy(u_hbm, z.at[inner], lsem.at[1])
     cp_r = pltpu.make_async_copy(f_hbm, r.at[inner], lsem.at[2])
     cp_u = pltpu.make_async_copy(u_hbm, u, lsem.at[3])
-    for cp in (cp_k, cp_z, cp_r):
+    for cp in (cp_z, cp_r):
         cp.start()
 
     def load_s(i):
@@ -86,25 +86,38 @@
     def load_r(i):
         return pltpu.make_async_copy(m_hbm.at[pl.ds(STRIP * i, STRIP), pl.ds(gc, REST)], mr.at[pl.ds(STRIP * i, STRIP)], msem.at[4 + i])
 
+    for a in (7, END):
+        z[a] = jnp.zeros((EXT, RHS), F32)
+    bar = pltpu.get_barrier_semaphore()
+    pl.semaphore_signal(bar, inc=1, device_id=ydev, device_id_type=MESH)
+    for d in SIDES:
+        def greet(d=d):
+            pl.semaphore_signal(bar, inc=1, device_id=xdev(d), device_id_type=MESH)
+            pl.semaphore_signal(bar, inc=1, device_id=ddev(d), device_id_type=MESH)
+        on_side(d, greet)
+    r[7] = jnp.zeros((EXT, RHS), F32)
+    r[END] = jnp.zeros((EXT, RHS), F32)
     for ref in (z, r):
-        ref[0:MG] = jnp.zeros((MG, EXT, RHS), F32)
-        ref[END:EXT] = jnp.zeros((MG, EXT, RHS), F32)
+        ref[0:7] = jnp.zeros((7, EXT, RHS), F32)
+        ref[57:EXT] = jnp.zeros((7, EXT, RHS), F32)
         ref[MG:END, 0:MG] = jnp.zeros((TILE, MG, RHS), F32)
         ref[MG:END, END:EXT] = jnp.zeros((TILE, MG, RHS), F32)
+
     kfull[...] = jnp.zeros_like(kfull)
-    ys[...] = jnp.zeros_like(ys)
-
-    bar = pltpu.get_barrier_semaphore()
-    pl.semaphore_signal(bar, inc=1, device_id=ydev, device_id_type=MESH)
-    for d in SIDES:
-        @pl.when(has[d])
-        def _(d=d):
-            pl.semaphore_signal(bar, inc=1, device_id=xdev(d), device_id_type=MESH)
-            pl.semaphore_signal(bar, inc=1, device_id=ddev(d), device_id_type=MESH)
+    kfull[MG:END, MG:END] = kown[...]
+    kt = kfull[...].T
+    prev = jnp.broadcast_to(kt[0:EXT, 7:MG], (EXT, 128))
+    for a in range(MG, 57):
+        here = jnp.broadcast_to(kt[0:EXT, a:a + 1], (EXT, 128))
+        wx[a - MG] = 0.5 * (prev + here)
+        if a < END:
+            wy[a - MG] = 0.5 * (pltpu.roll(here, 1, 0) + here)
+        prev = here
+    for k in range(TILE):
+        wy[k, pl.ds(face, 1), :] = jnp.zeros((1, 128), F32)
     n_sides = has_up.astype(jnp.int32) + has_dn.astype(jnp.int32)
     pl.semaphore_wait(bar, 1 + 2 * n_sides)
 
-    cp_k.wait()
     k_y = remote(kown, krecv.at[2], ie_s.at[0], ie_r.at[0], ydev)
     k_y.start()
     k_x = [remote(kown, krecv.at[1 - d], ie_s.at[1 + d], ie_r.at[2 - d], xdev(d)) for d in SIDES]
@@ -125,36 +138,11 @@
     cp_r.wait()
     for i in range(4):
         load_s(i).start()
-    for i in range(4):
+    load_r(3 * first).start()
+    load_r(3 - 3 * first).start()
+    for i in (1, 2):
         load_r(i).start()
     cp_u.start()
-
-    kfull[MG:END, MG:END] = kown[...]
-    for d in SIDES:
-        @pl.when(has[d])
-        def _(d=d):
-            k_in[d].wait_recv()
-            src = 47 if d == 0 else 0
-            dst = 7 if d == 0 else END
-            kfull[dst:dst + 1, MG:END] = krecv[d, src:src + 1, :]
-    k_y.wait_recv()
-
-    @pl.when(col == 0)
-    def _():
-        kfull[MG:END, END:57] = krecv[2, :, 0:1]
-
-    @pl.when(col == 1)
-    def _():
-        kfull[MG:END, 7:MG] = krecv[2, :, 47:TILE]
-
-    kt = kfull[...].T
-    prev = jnp.broadcast_to(kt[0:EXT, 7:MG], (EXT, 128))
-    for a in range(MG, 57):
-        here = jnp.broadcast_to(kt[0:EXT, a:a + 1], (EXT, 128))
-        wx[a - MG] = 0.5 * (prev + here)
-        if a < END:
-            wy[a - MG] = 0.5 * (pltpu.roll(here, 1, 0) + here)
-        prev = here
 
     def both(v):
         return jnp.concatenate([v, v], axis=1)
@@ -245,6 +233,17 @@
             return carry
         lax.fori_loop(0, n, body, 0)
 
+    def recv_side(d):
+        rx_in(d).wait_recv()
+        rd_in(d).wait_recv()
+        for i in range(MG):
+            r[END * d + i, MG:END, :] = rrx[d, i].astype(F32)
+        for q in range(4):
+            v = rrd[d, q].astype(F32)
+            r[END * d + 2 * q, pl.ds(hc, MG), :] = v[0:MG]
+            r[END * d + 2 * q + 1, pl.ds(hc, MG), :] = v[MG:STRIP]
+        to_w(END * d, MG, 0, EXT)
+
     def recv_r():
         to_w(MG, TILE, rc, TILE)
         ry_early().wait_recv()
@@ -254,17 +253,7 @@
             on_side(d, lambda d=d: pl.when(same_chip(d))(lambda: rd_forward(d).start()))
             unpack_ry(17 * d, 7)
         for d in (order[1], order[0]):
-            def side(d=d):
-                rx_in(d).wait_recv()
-                rd_in(d).wait_recv()
-                for i in range(MG):
-                    r[END * d + i, MG:END, :] = rrx[d, i].astype(F32)
-                for q in range(4):
-                    v = rrd[d, q].astype(F32)
-                    r[END * d + 2 * q, pl.ds(hc, MG), :] = v[0:MG]
-                    r[END * d + 2 * q + 1, pl.ds(hc, MG), :] = v[MG:STRIP]
-                to_w(END * d, MG, 0, EXT)
-            on_side(d, side)
+            on_side(d, lambda d=d: recv_side(d))
         ry_mid().wait_recv()
         unpack_ry(*RMID)
         ry_mid().wait_send()
@@ -277,35 +266,83 @@
                 rd(d).wait_send()
             on_side(d, sent)
 
-    for d in SIDES:
-        @pl.when(has[d])
-        def _(d=d):
+    update(9, 46, cd, STRIP, 1.0, False)
+    pack_ry(1, 22)
+    ry(1, 22, 2).start()
+    update(9, 46, ci, 32, 1.0, False)
+    for d in SIDES:
+        def edge(d=d):
+            k_in[d].wait_recv()
+            kfull[7 + 49 * d:MG + 49 * d, MG:END] = krecv[d, 47 - 47 * d:TILE - 47 * d, :]
             u_in[d].wait_recv()
+        on_side(d, edge)
+    kt = kfull[...].T
+    for d in SIDES:
+        a = MG + TILE * d
+        wx[TILE * d] = 0.5 * (jnp.broadcast_to(kt[0:EXT, a - 1:a], (EXT, 128))
+                              + jnp.broadcast_to(kt[0:EXT, a:a + 1], (EXT, 128)))
+    for d in SIDES:
+        update(MG + 47 * d, 1, cd, STRIP, 1.0, False)
+        pack_ry(23 * d, 1)
+        ry(23 * d, 1, d).start()
+    for k in range(TILE):
+        pcs[k // MG, k % MG, :] = r[MG + k, pl.ds(es, 1), :][0]
+    p_y = remote(pcs, pcr, ie_s.at[6], ie_r.at[6], ydev)
+    p_y.start()
+    for d in SIDES:
+        update(MG + 47 * d, 1, ci, 32, 1.0, False)
+    k_y.wait_recv()
     u_y.wait_recv()
+
+    def lane(ref, i):
+        return jnp.broadcast_to(ref[:, i:i + 1], (TILE, 128))
+
+    k_nb = krecv[2]
+    k_me = kown[...]
+    wf = 0.5 * (jnp.where(col == 0, lane(k_me, 47), lane(k_me, 0))
+                + jnp.where(col == 0, lane(k_nb, 0), lane(k_nb, 47)))
+    flux = both(wf) * (ues[...].reshape(TILE, RHS) - uer[...].reshape(TILE, RHS))
+    mine = pcs[...].reshape(TILE, RHS) - flux
     for k in range(TILE):
-        z[MG + k, pl.ds(er, 1), :] = uer[k // MG, k % MG, :][None]
-    for d in SIDES:
-        update(MG + 34 * d, 14, cd, STRIP, 1.0, False)
-    for d in SIDES:
-        send_ry_side(d)
-    update(22, 20, cd, STRIP, 1.0, False)
-    send_ry_early()
-    send_ry_mid()
-    update(MG, MG, ci, 32, 1.0, False)
-    update(TILE, MG, ci, 32, 1.0, False)
-    for d in SIDES:
+        wy[k, pl.ds(face, 1), :] = wf[k:k + 1]
+        r[MG + k, pl.ds(es, 1), :] = mine[k:k + 1]
+
+    def corner(d):
+        return remote(rdb.at[d], rrd.at[1 - d], rd_s.at[d], rd_r.at[1 - d], ddev(d))
+
+    for d in SIDES:
+        for q in range(4):
+            a = MG + REST * d + 2 * q
+            rdb[d, q] = jnp.concatenate([r[a, pl.ds(mc, MG), :], r[a + 1, pl.ds(mc, MG), :]], axis=0).astype(BF16)
+        on_side(d, lambda d=d: corner(d).start())
         send_rx(d)
         off_side(d, lambda d=d: to_w(END * d, MG, 0, EXT))
-    update(STRIP, 32, ci, 32, 1.0, False)
-    recv_r()
+    to_w(MG, TILE, rc, TILE)
+    for d in SIDES:
+        ry(23 * d, 1, d).wait_recv()
+        unpack_ry(23 * d, 1)
+    ry(1, 22, 2).wait_recv()
+    unpack_ry(1, 22)
+    p_y.wait_recv()
+    theirs = pcr[...].reshape(TILE, RHS) + flux
+    for k in range(TILE):
+        r[MG + k, pl.ds(er, 1), :] = theirs[k:k + 1]
+    to_w(MG, TILE, sc, STRIP)
+    for d in (order[1], order[0]):
+        on_side(d, lambda d=d: recv_side(d))
+    ry(1, 22, 2).wait_send()
+    for d in SIDES:
+        ry(23 * d, 1, d).wait_send()
+
+        def sent(d=d):
+            k_x[d].wait_send()
+            u_x[d].wait_send()
+            rx(d).wait_send()
+            corner(d).wait_send()
+        on_side(d, sent)
     k_y.wait_send()
     u_y.wait_send()
-    for d in SIDES:
-        @pl.when(has[d])
-        def _(d=d):
-            k_x[d].wait_send()
-            u_x[d].wait_send()
-    cp_u.wait()
+    p_y.wait_send()
 
     om = omega[0]
 
@@ -413,12 +450,9 @@
             return c
         lax.fori_loop(0, 2, ends_s, 0)
 
-        @pl.when(s == 0)
-        def _():
-            for i in range(4):
-                load_r(i).wait()
         def ends_r(i, c):
             d = jnp.where(i == 0, first, 1 - first)
+            pl.when(s == 0)(lambda: load_r(3 * d).wait())
             dot_r(TILE * d)
             on_side(d, lambda: xr(d).start())
             off_side(d, lambda: no_row_r(d))
@@ -427,7 +461,13 @@
             return c
         lax.fori_loop(0, 2, ends_r, 0)
         send_y(2)
-        lax.fori_loop(1, 3, lambda i, c: (dot_r(STRIP * i), c)[1], 0)
+
+        def mid_r(i, c):
+            pl.when(s == 0)(lambda: load_r(i).wait())
+            dot_r(STRIP * i)
+            return c
+        lax.fori_loop(1, 3, mid_r, 0)
+        pl.when(s == 0)(lambda: cp_u.wait())
         recv_y(0)
         update(22, MG, cd, STRIP, om, True)
         send_ry_early()
@@ -563,7 +603,8 @@
         return pl.pallas_call(
             kernel,
             out_shape=jax.ShapeDtypeStruct((TILE, TILE, RHS), F32),
-            in_specs=[pl.BlockSpec(memory_space=pltpu.SMEM)] + [any_spec] * 4,
+            in_specs=[pl.BlockSpec(memory_space=pltpu.SMEM), any_spec, any_spec,
+                      pl.BlockSpec(memory_space=pltpu.VMEM), any_spec],
             out_specs=pl.BlockSpec(memory_space=pltpu.VMEM),
             scratch_shapes=[
                 pltpu.VMEM((EXT, STRIP, WIN), BF16),
@@ -573,7 +614,6 @@
                 pltpu.VMEM((EXT, EXT, RHS), F32),
                 pltpu.VMEM((49, EXT, 128), F32),
                 pltpu.VMEM((TILE, EXT, 128), F32),
-                pltpu.VMEM((TILE, TILE), F32),
                 pltpu.VMEM((3, TILE, TILE), F32),
                 pltpu.VMEM((128, 128), F32),
                 pltpu.VMEM((YLEN, MG, RHS), F32),
@@ -585,6 +625,9 @@
                 pltpu.VMEM((2, MG, TILE, RHS), BF16),
                 pltpu.VMEM((2, MG, TILE, RHS), BF16),
                 pltpu.VMEM((2, 4, STRIP, RHS), BF16),
+                pltpu.VMEM((2, 4, STRIP, RHS), BF16),
+                pltpu.VMEM((6, MG, RHS), F32),
+                pltpu.VMEM((6, MG, RHS), F32),
                 pltpu.VMEM((6, MG, RHS), F32),
                 pltpu.VMEM((6, MG, RHS), F32),
                 pltpu.VMEM((24, STRIP, RHS), BF16),
@@ -595,7 +638,7 @@
                 pltpu.VMEM((2, 4, 80, RHS), BF16),
                 dma((5,)), dma((5,)), dma((2,)), dma((2,)), dma((2,)), dma((2,)),
                 dma((4,)), dma((4,)), dma((2,)), dma((2,)), dma((2,)), dma((2,)),
-                dma((6,)), dma((6,)), dma((4,)), dma((4,)), dma((4,)), dma((4,)), dma((4,)), dma((MG,)),
+                dma((7,)), dma((7,)), dma((4,)), dma((4,)), dma((4,)), dma((4,)), dma((4,)), dma((MG,)),
             ],
             compiler_params=pltpu.CompilerParams(
                 collective_id=0, has_side_effects=True, vmem_limit_bytes=54_000_000),

time: 83.8 us -> 82 us (0.979)
  Pallas kernels: 80.9 us -> 79.1 us
    pallas_call x1, Pallas kernels: 80.9 us -> 79.1 us  [local_step(): pl.pallas_call(kernel, out_shape=jax.ShapeDtypeStruct((TILE, TILE, RHS),...]
where the time goes in v6:
time: 82 us; the launch traced here: 81.9 us
  Pallas kernels  79.1 us (96%)
  local copies, waits for them, and re-layouts  2.14 us (3%)
    pallas_call x1, Pallas kernels, local_step(): pl.pallas_call(kernel, out_shape=jax.ShapeDtypeStruct((TILE, TILE, RHS),...  79.1 us
    unnamed x3, local copies, waits for them, and re-layouts  2.14 us

profile of v6, /device:TPU:0, one launch (start us, length us, event | category | flops | bytes accessed | tf_op | source)
XLA Modules:
  0.0 81.9 jit_solution(5131224284181785314)
XLA Ops:
  0.7 0.0 copy-start
  0.7 0.7 copy-done
  1.4 79.1 %schwarz.1 = f32[48,48,256]{2,1,0:T(8,128)S(1)} custom-call(f32[1]{0:T(128)} %bitcast.2.omega, f32[48,48,256]{2,1,0:T(8,128)} %f_hbm.1, f32[48,48,256]{2,1,0:T(8,128)} %u_hbm.1, f32[48,48]{1,0:T(8,128)S(1)} %copy-done, bf16[64,64,4096]{2,1,0:T(8,128)(2,1)} %bitcast.3), custom_call_target="tpu_custom_call" | custom-call | tf_op jit(solution)/shard_map/schwarz/pallas_call | solution.py:603
  80.4 1.4 %copy.8 = f32[48,48,256]{2,1,0:T(8,128)} copy(f32[48,48,256]{2,1,0:T(8,128)S(1)} %schwarz.1) | data formatting | bytes 4718592
Async XLA Ops:
  0.7 0.7 copy-start

commit v7 on v6

--- a/solution.py
+++ b/solution.py
@@ -16,6 +16,10 @@
 STRIP = 16
 REST = 40
 END = 56
+END_ROWS = 640
+LATE = 768
+LANES = 128
+GROUP = 1024
 SIDES = (0, 1)
 F32 = jnp.float32
 BF16 = jnp.bfloat16
@@ -31,7 +35,7 @@
 def kernel(omega, f_hbm, u_hbm, kown, m_hbm, u,
            ms, mr, w, z, r, wx, wy, krecv, kfull,
            ys, yr, xrs, xrr, rsy, rry, rsx, rrx, rrd, rdb, ues, uer, pcs, pcr,
-           fys, fyr_, fxs, fxsr, fxr, fxrr,
+           fys, fyr_, fxs, fxsr, fxr, fxrr, msl, wl, psel,
            yz_s, yz_r, xs_s, xs_r, xr_s, xr_r, ry_s, ry_r, rx_s, rx_r, rd_s, rd_r,
            ie_s, ie_r, fy_s, fy_r, fx_s, fx_r, lsem, msem):
     col = lax.axis_index("col")
@@ -106,15 +110,15 @@
     kfull[...] = jnp.zeros_like(kfull)
     kfull[MG:END, MG:END] = kown[...]
     kt = kfull[...].T
-    prev = jnp.broadcast_to(kt[0:EXT, 7:MG], (EXT, 128))
+    prev = jnp.broadcast_to(kt[0:EXT, 7:MG], (EXT, LANES))
     for a in range(MG, 57):
-        here = jnp.broadcast_to(kt[0:EXT, a:a + 1], (EXT, 128))
+        here = jnp.broadcast_to(kt[0:EXT, a:a + 1], (EXT, LANES))
         wx[a - MG] = 0.5 * (prev + here)
         if a < END:
             wy[a - MG] = 0.5 * (pltpu.roll(here, 1, 0) + here)
         prev = here
     for k in range(TILE):
-        wy[k, pl.ds(face, 1), :] = jnp.zeros((1, 128), F32)
+        wy[k, pl.ds(face, 1), :] = jnp.zeros((1, LANES), F32)
     n_sides = has_up.astype(jnp.int32) + has_dn.astype(jnp.int32)
     pl.semaphore_wait(bar, 1 + 2 * n_sides)
 
@@ -163,6 +167,52 @@
             return carry
         lax.fori_loop(0, rows, body, 0)
 
+    lo, hi = MG * EXT, END * EXT
+
+    def pack_late(lhs, dst, row0, rows):
+        for g in range(3):
+            cols = lhs[:, lo + GROUP * g:lo + GROUP * (g + 1)]
+            dst[pl.ds(row0, rows), RHS * g:RHS * (g + 1)] = jnp.dot(
+                cols, psel[...], preferred_element_type=F32).astype(BF16)
+
+    def pack_matrix():
+        k = lax.broadcasted_iota(jnp.int32, (GROUP, RHS), 0)
+        n = lax.broadcasted_iota(jnp.int32, (GROUP, RHS), 1)
+        hit = ((k >> 6) == (n >> 4)) & ((k & 63) == sc + (n & 15))
+        psel[...] = jnp.where(hit, 1.0, 0.0).astype(BF16)
+
+        def strip(i, c):
+            load_s(i).wait()
+            pack_late(ms[pl.ds(STRIP * i, STRIP)].reshape(RHS, WIN), msl, pl.multiple_of(RHS * i, RHS), RHS)
+            return c
+        lax.fori_loop(0, 4, strip, 0)
+
+    def early_s():
+        w[MG:END, pl.ds(sc, STRIP), :] = jnp.zeros((TILE, STRIP, RHS), BF16)
+
+        def strip(i, c):
+            lhs = ms[pl.ds(STRIP * i, STRIP)].reshape(RHS, WIN)[:, lo:hi]
+            z[pl.ds(STRIP * i, STRIP), pl.ds(sc, STRIP), :] = jnp.dot(
+                lhs, w[MG:END].reshape(hi - lo, RHS), preferred_element_type=F32).reshape(STRIP, STRIP, RHS)
+            return c
+        lax.fori_loop(0, 4, strip, 0)
+
+    def late(lhs, packed):
+        cells = jnp.concatenate([w[0:MG].reshape(lo, RHS), w[END:EXT].reshape(lo, RHS),
+                                 wl[...].reshape(LATE, RHS)], axis=0)
+        return jnp.dot(jnp.concatenate([lhs[:, 0:lo], lhs[:, hi:WIN], packed], axis=1), cells,
+                       preferred_element_type=F32)
+
+    def dot_s(a0):
+        part = late(ms[pl.ds(a0, STRIP)].reshape(RHS, WIN), msl[pl.ds(pl.multiple_of(a0 * STRIP, RHS), RHS), :])
+        here = (pl.ds(a0, STRIP), pl.ds(sc, STRIP))
+        z[here] = z[here] + part.reshape(STRIP, STRIP, RHS)
+
+    def dot_r(a0):
+        lhs = mr[pl.ds(a0, STRIP)].reshape(END_ROWS, WIN)
+        z[pl.ds(a0, STRIP), pl.ds(gc, REST), :] = jnp.dot(
+            lhs, w[...].reshape(WIN, RHS), preferred_element_type=F32).reshape(STRIP, REST, RHS)
+
     def ry(p0, n, j):
         return remote(rsy.at[pl.ds(p0, n)], rry.at[pl.ds(p0, n)], ry_s.at[j], ry_r.at[j], ydev)
 
@@ -221,6 +271,11 @@
             w[a0 + i, pl.ds(c0, n), :] = r[a0 + i, pl.ds(c0, n), :].astype(BF16)
             return carry
         lax.fori_loop(0, rows, body, 0)
+
+    def to_strip(a):
+        cells = r[a, pl.ds(sc, STRIP), :].astype(BF16)
+        w[a, pl.ds(sc, STRIP), :] = cells
+        wl[a - MG] = cells
 
     def unpack_ry(p0, n):
         def body(i, carry):
@@ -228,8 +283,8 @@
             a = MG + 2 * (p0 + i)
             r[a, pl.ds(hc, MG), :] = v[0:MG]
             r[a + 1, pl.ds(hc, MG), :] = v[MG:STRIP]
-            w[a, pl.ds(sc, STRIP), :] = r[a, pl.ds(sc, STRIP), :].astype(BF16)
-            w[a + 1, pl.ds(sc, STRIP), :] = r[a + 1, pl.ds(sc, STRIP), :].astype(BF16)
+            to_strip(a)
+            to_strip(a + 1)
             return carry
         lax.fori_loop(0, n, body, 0)
 
@@ -246,6 +301,7 @@
 
     def recv_r():
         to_w(MG, TILE, rc, TILE)
+        early_s()
         ry_early().wait_recv()
         unpack_ry(*REARLY)
         for d in (order[1], order[0]):
@@ -279,8 +335,8 @@
     kt = kfull[...].T
     for d in SIDES:
         a = MG + TILE * d
-        wx[TILE * d] = 0.5 * (jnp.broadcast_to(kt[0:EXT, a - 1:a], (EXT, 128))
-                              + jnp.broadcast_to(kt[0:EXT, a:a + 1], (EXT, 128)))
+        wx[TILE * d] = 0.5 * (jnp.broadcast_to(kt[0:EXT, a - 1:a], (EXT, LANES))
+                              + jnp.broadcast_to(kt[0:EXT, a:a + 1], (EXT, LANES)))
     for d in SIDES:
         update(MG + 47 * d, 1, cd, STRIP, 1.0, False)
         pack_ry(23 * d, 1)
@@ -295,7 +351,7 @@
     u_y.wait_recv()
 
     def lane(ref, i):
-        return jnp.broadcast_to(ref[:, i:i + 1], (TILE, 128))
+        return jnp.broadcast_to(ref[:, i:i + 1], (TILE, LANES))
 
     k_nb = krecv[2]
     k_me = kown[...]
@@ -318,6 +374,10 @@
         send_rx(d)
         off_side(d, lambda d=d: to_w(END * d, MG, 0, EXT))
     to_w(MG, TILE, rc, TILE)
+    pack_matrix()
+    for d in SIDES:
+        on_side(d, lambda d=d: u_x[d].wait_send())
+    early_s()
     for d in SIDES:
         ry(23 * d, 1, d).wait_recv()
         unpack_ry(23 * d, 1)
@@ -327,7 +387,11 @@
     theirs = pcr[...].reshape(TILE, RHS) + flux
     for k in range(TILE):
         r[MG + k, pl.ds(er, 1), :] = theirs[k:k + 1]
-    to_w(MG, TILE, sc, STRIP)
+
+    def strip_row(i, c):
+        to_strip(MG + i)
+        return c
+    lax.fori_loop(0, TILE, strip_row, 0)
     for d in (order[1], order[0]):
         on_side(d, lambda d=d: recv_side(d))
     ry(1, 22, 2).wait_send()
@@ -336,7 +400,6 @@
 
         def sent(d=d):
             k_x[d].wait_send()
-            u_x[d].wait_send()
             rx(d).wait_send()
             corner(d).wait_send()
         on_side(d, sent)
@@ -345,16 +408,6 @@
     p_y.wait_send()
 
     om = omega[0]
-
-    def dot_s(a0):
-        lhs = ms[pl.ds(a0, STRIP)].reshape(RHS, WIN)
-        z[pl.ds(a0, STRIP), pl.ds(sc, STRIP), :] = jnp.dot(
-            lhs, w[...].reshape(WIN, RHS), preferred_element_type=F32).reshape(STRIP, STRIP, RHS)
-
-    def dot_r(a0):
-        lhs = mr[pl.ds(a0, STRIP)].reshape(640, WIN)
-        z[pl.ds(a0, STRIP), pl.ds(gc, REST), :] = jnp.dot(
-            lhs, w[...].reshape(WIN, RHS), preferred_element_type=F32).reshape(STRIP, REST, RHS)
 
     def yz(j, off, length):
         return remote(ys.at[pl.ds(off, length)], yr.at[pl.ds(off, length)], yz_s.at[j], yz_r.at[j], ydev)
@@ -433,10 +486,6 @@
         z[7 + 49 * d, pl.ds(gc, REST), :] = jnp.zeros((REST, RHS), F32)
 
     def sweep(s, carry):
-        @pl.when(s == 0)
-        def _():
-            for i in range(4):
-                load_s(i).wait()
         dot_s(STRIP)
         send_y(0)
         dot_s(32)
@@ -612,10 +661,10 @@
                 pltpu.VMEM((EXT, EXT, RHS), BF16),
                 pltpu.VMEM((EXT, EXT, RHS), F32),
                 pltpu.VMEM((EXT, EXT, RHS), F32),
-                pltpu.VMEM((49, EXT, 128), F32),
-                pltpu.VMEM((TILE, EXT, 128), F32),
+                pltpu.VMEM((49, EXT, LANES), F32),
+                pltpu.VMEM((TILE, EXT, LANES), F32),
                 pltpu.VMEM((3, TILE, TILE), F32),
-                pltpu.VMEM((128, 128), F32),
+                pltpu.VMEM((LANES, LANES), F32),
                 pltpu.VMEM((YLEN, MG, RHS), F32),
                 pltpu.VMEM((YLEN, MG, RHS), F32),
                 pltpu.VMEM((2, 9, STRIP, RHS), F32),
@@ -636,12 +685,15 @@
                 pltpu.VMEM((2, MG, STRIP, RHS), BF16),
                 pltpu.VMEM((2, 4, 80, RHS), BF16),
                 pltpu.VMEM((2, 4, 80, RHS), BF16),
+                pltpu.VMEM((GROUP, LATE), BF16),
+                pltpu.VMEM((TILE, STRIP, RHS), BF16),
+                pltpu.VMEM((GROUP, RHS), BF16),
                 dma((5,)), dma((5,)), dma((2,)), dma((2,)), dma((2,)), dma((2,)),
                 dma((4,)), dma((4,)), dma((2,)), dma((2,)), dma((2,)), dma((2,)),
                 dma((7,)), dma((7,)), dma((4,)), dma((4,)), dma((4,)), dma((4,)), dma((4,)), dma((MG,)),
             ],
             compiler_params=pltpu.CompilerParams(
-                collective_id=0, has_side_effects=True, vmem_limit_bytes=54_000_000),
+                collective_id=0, has_side_effects=True, vmem_limit_bytes=53_000_000),
             name="schwarz",
         )(relax_omega.reshape(1), forcing, u_init, diffusivity,
           local_solve.reshape(EXT, EXT, WIN))

time: 82 us -> 78.9 us (0.962)
  Pallas kernels: 79.1 us -> 76 us
    pallas_call x1, Pallas kernels: 79.1 us -> 76 us  [local_step(): pl.pallas_call(kernel, out_shape=jax.ShapeDtypeStruct((TILE, TILE, RHS),...]
where the time goes in v7:
time: 78.9 us; the launch traced here: 78.8 us
  Pallas kernels  76 us (96%)
  local copies, waits for them, and re-layouts  2.14 us (3%)
    pallas_call x1, Pallas kernels, local_step(): pl.pallas_call(kernel, out_shape=jax.ShapeDtypeStruct((TILE, TILE, RHS),...  76 us
    unnamed x3, local copies, waits for them, and re-layouts  2.14 us

profile of v7, /device:TPU:0, one launch (start us, length us, event | category | flops | bytes accessed | tf_op | source)
XLA Modules:
  0.0 78.8 jit_solution(489371216813698315)
XLA Ops:
  0.7 0.0 copy-start
  0.7 0.7 copy-done
  1.4 76.0 %schwarz.1 = f32[48,48,256]{2,1,0:T(8,128)S(1)} custom-call(f32[1]{0:T(128)} %bitcast.2.omega, f32[48,48,256]{2,1,0:T(8,128)} %f_hbm.1, f32[48,48,256]{2,1,0:T(8,128)} %u_hbm.1, f32[48,48]{1,0:T(8,128)S(1)} %copy-done, bf16[64,64,4096]{2,1,0:T(8,128)(2,1)} %bitcast.3), custom_call_target="tpu_custom_call" | custom-call | tf_op jit(solution)/shard_map/schwarz/pallas_call | solution.py:652
  77.4 1.4 %copy.8 = f32[48,48,256]{2,1,0:T(8,128)} copy(f32[48,48,256]{2,1,0:T(8,128)S(1)} %schwarz.1) | data formatting | bytes 4718592
Async XLA Ops:
  0.7 0.7 copy-start

commit v8 on v7

--- a/solution.py
+++ b/solution.py
@@ -32,8 +32,8 @@
 REARLY = (7, 4)
 FCHUNKS = ((4, MG), (12, MG))
 
-def kernel(omega, f_hbm, u_hbm, kown, m_hbm, u,
-           ms, mr, w, z, r, wx, wy, krecv, kfull,
+def kernel(omega, f_hbm, u_hbm, kap_hbm, m_hbm, u,
+           ms, mr, w, z, r, wx, wy, kown, krecv, kfull,
            ys, yr, xrs, xrr, rsy, rry, rsx, rrx, rrd, rdb, ues, uer, pcs, pcr,
            fys, fyr_, fxs, fxsr, fxr, fxrr, msl, wl, psel,
            yz_s, yz_r, xs_s, xs_r, xr_s, xr_r, ry_s, ry_r, rx_s, rx_r, rd_s, rd_r,
@@ -81,7 +81,8 @@
     cp_z = pltpu.make_async_copy(u_hbm, z.at[inner], lsem.at[1])
     cp_r = pltpu.make_async_copy(f_hbm, r.at[inner], lsem.at[2])
     cp_u = pltpu.make_async_copy(u_hbm, u, lsem.at[3])
-    for cp in (cp_z, cp_r):
+    cp_k = pltpu.make_async_copy(kap_hbm, kown, lsem.at[0])
+    for cp in (cp_k, cp_z, cp_r):
         cp.start()
 
     def load_s(i):
@@ -108,6 +109,7 @@
         ref[MG:END, END:EXT] = jnp.zeros((TILE, MG, RHS), F32)
 
     kfull[...] = jnp.zeros_like(kfull)
+    cp_k.wait()
     kfull[MG:END, MG:END] = kown[...]
     kt = kfull[...].T
     prev = jnp.broadcast_to(kt[0:EXT, 7:MG], (EXT, LANES))
@@ -653,7 +655,7 @@
             kernel,
             out_shape=jax.ShapeDtypeStruct((TILE, TILE, RHS), F32),
             in_specs=[pl.BlockSpec(memory_space=pltpu.SMEM), any_spec, any_spec,
-                      pl.BlockSpec(memory_space=pltpu.VMEM), any_spec],
+                      any_spec, any_spec],
             out_specs=pl.BlockSpec(memory_space=pltpu.VMEM),
             scratch_shapes=[
                 pltpu.VMEM((EXT, STRIP, WIN), BF16),
@@ -663,6 +665,7 @@
                 pltpu.VMEM((EXT, EXT, RHS), F32),
                 pltpu.VMEM((49, EXT, LANES), F32),
                 pltpu.VMEM((TILE, EXT, LANES), F32),
+                pltpu.VMEM((TILE, TILE), F32),
                 pltpu.VMEM((3, TILE, TILE), F32),
                 pltpu.VMEM((LANES, LANES), F32),
                 pltpu.VMEM((YLEN, MG, RHS), F32),
@@ -695,7 +698,8 @@
             compiler_params=pltpu.CompilerParams(
                 collective_id=0, has_side_effects=True, vmem_limit_bytes=53_000_000),
             name="schwarz",
-        )(relax_omega.reshape(1), forcing, u_init, diffusivity,
+        )(relax_omega.reshape(1), forcing, u_init,
+          pltpu.with_memory_space_constraint(diffusivity, pltpu.HBM),
           local_solve.reshape(EXT, EXT, WIN))
 
     field_spec = P('row', 'col', None)

time: 78.9 us -> 78.2 us (level)
    unnamed x3 -> x1, local copies, waits for them, and re-layouts: 2.14 us -> 1.41 us
where the time goes in v8:
time: 78.2 us; the launch traced here: 78.1 us
  Pallas kernels  76.1 us (97%)
  local copies, waits for them, and re-layouts  1.41 us (2%)
    pallas_call x1, Pallas kernels, local_step(): pl.pallas_call(kernel, out_shape=jax.ShapeDtypeStruct((TILE, TILE, RHS),...  76.1 us

profile of v8, /device:TPU:0, one launch (start us, length us, event | category | flops | bytes accessed | tf_op | source)
XLA Modules:
  0.0 78.1 jit_solution(6843183028719092225)
XLA Ops:
  0.7 76.1 %schwarz.1 = f32[48,48,256]{2,1,0:T(8,128)S(1)} custom-call(f32[1]{0:T(128)} %bitcast.2.omega, f32[48,48,256]{2,1,0:T(8,128)} %f_hbm.1, f32[48,48,256]{2,1,0:T(8,128)} %u_hbm.1, f32[48,48]{1,0:T(8,128)} %kap_hbm.1, bf16[64,64,4096]{2,1,0:T(8,128)(2,1)} %bitcast.3), custom_call_target="tpu_custom_call" | custom-call | tf_op jit(solution)/shard_map/schwarz/pallas_call | solution.py:654
  76.7 1.4 %copy.8 = f32[48,48,256]{2,1,0:T(8,128)} copy(f32[48,48,256]{2,1,0:T(8,128)S(1)} %schwarz.1) | data formatting | bytes 4718592

commit v9 on v8

--- a/solution.py
+++ b/solution.py
@@ -629,10 +629,21 @@
         send_fy(3 - d, 20 * (1 - d), 4)
         return c
     lax.fori_loop(0, 2, last_ends_r, 0)
-    lax.fori_loop(1, 3, lambda i, c: (dot_r(STRIP * i), c)[1], 0)
+    def last_mid(i, c):
+        part = jnp.dot(mr[pl.ds(STRIP * i, STRIP)].reshape(END_ROWS, WIN), w[...].reshape(WIN, RHS),
+                       preferred_element_type=F32).reshape(STRIP, REST, RHS)
+        here = (pl.ds(STRIP * i - MG, STRIP), pl.ds(gc - MG, REST))
+        u[here] = u[here] + om * part
+        return c
+    lax.fori_loop(1, 3, last_mid, 0)
     for j in SIDES:
         last_y(j, *FCHUNKS[j])
-    add_u(STRIP, 32)
+
+    def add_strip(i, c):
+        here = pl.ds(mc - MG, MG)
+        u[MG + i, here, :] = u[MG + i, here, :] + om * z[STRIP + i, pl.ds(mc, MG), :]
+        return c
+    lax.fori_loop(0, 32, add_strip, 0)
     for d in (order[1], order[0]):
         on_side(d, lambda d=d: last_fold_r(d))
         last_y(2 + d, 20 * d, 4)

time: 78.2 us -> 78.2 us (level)
  no operation moved by 1% of the time
where the time goes in v9:
time: 78.2 us; the launch traced here: 78.1 us
  Pallas kernels  76 us (97%)
  local copies, waits for them, and re-layouts  1.41 us (2%)
    pallas_call x1, Pallas kernels, local_step(): pl.pallas_call(kernel, out_shape=jax.ShapeDtypeStruct((TILE, TILE, RHS),...  76 us

profile of v9, /device:TPU:0, one launch (start us, length us, event | category | flops | bytes accessed | tf_op | source)
XLA Modules:
  0.0 78.1 jit_solution(3284351040841082424)
XLA Ops:
  0.7 76.0 %schwarz.1 = f32[48,48,256]{2,1,0:T(8,128)S(1)} custom-call(f32[1]{0:T(128)} %bitcast.2.omega, f32[48,48,256]{2,1,0:T(8,128)} %f_hbm.1, f32[48,48,256]{2,1,0:T(8,128)} %u_hbm.1, f32[48,48]{1,0:T(8,128)} %kap_hbm.1, bf16[64,64,4096]{2,1,0:T(8,128)(2,1)} %bitcast.3), custom_call_target="tpu_custom_call" | custom-call | tf_op jit(solution)/shard_map/schwarz/pallas_call | solution.py:665
  76.7 1.4 %copy.8 = f32[48,48,256]{2,1,0:T(8,128)} copy(f32[48,48,256]{2,1,0:T(8,128)S(1)} %schwarz.1) | data formatting | bytes 4718592
